TPU v7x, 32 devices: a whole 2x2x4 slice. The times are simulated.
32 devices in a mesh: batch: 4 (over x, core), seq: 8 (over z, y).
Axes of the slice: x: 2, y: 2, z: 4, core: 2. Of those that a mesh axis runs over, the one named last changes fastest.
Arguments:
- layer_inputs: bfloat16 [25600, 800], P(('batch', 'seq')), may hold values from -24 to 24
- output_grads: bfloat16 [25600, 800], P(('batch', 'seq')), may hold values from -48 to 48
- input_inverse: float32 [800, 200], replicated, may hold values from -1 to 3
- output_inverse: float32 [800, 200], replicated, may hold values from -1 to 3
Outputs:
- input_factor: float32 [800, 200], P('seq')
- output_factor: float32 [800, 200], P('seq')
- preconditioned: bfloat16 [800, 800], replicated
All inputs are finite; a program needn't handle non-finite values.
Results may differ from a plain program's by a relative error of at most 0.0075.
Values may be sent and summed in bfloat16 or wider, within the bound.
No kernel may reach another device: no remote copies, remote signals or barrier semaphores. Data moves between devices by JAX's collectives and lax.ppermute only.
A program may use at most 64 MiB of HBM per device.

v0:
```python
import jax
import jax.numpy as jnp
from jax import lax
from jax.experimental import pallas as pl
from jax.experimental.pallas import tpu as pltpu
from jax.sharding import PartitionSpec as P


AXES = ("batch", "seq")
LANES = 128
PACK = 16
VMEM_LIMIT = 16 << 20
F32 = jnp.float32
BF16 = jnp.bfloat16
NN = (((1,), (0,)), ((), ()))
NT = (((1,), (1,)), ((), ()))


def dot(a, b, dims):
    return lax.dot_general(a, b, dims, preferred_element_type=F32)


def up(value, step):
    return -(-value // step) * step


class Plan:
    def __init__(self, tokens, width, block, nb, ns):
        self.tokens, self.width, self.block = tokens, width, block
        self.nb, self.ns = nb, ns
        self.blocks = width // block
        assert self.blocks == 4 and nb % 2 == 0 and nb >= 4 and ns >= 8
        assert LANES < block <= 2 * LANES and block % 8 == 0
        self.corner = block - LANES
        self.folds = []
        base, column = block, LANES
        while column < block:
            lanes = 1
            while column + 2 * lanes <= block:
                lanes *= 2
            rows = up(-(-block * lanes // LANES), 8)
            self.folds.append((column, lanes, base, rows))
            base, column = base + rows, column + lanes
        self.grad_rows = up(base, PACK)
        self.cov_total = up(block + self.corner, PACK)
        units = self.cov_total // PACK
        self.quarter = -(-units // 4)
        self.cuts = [min(units, self.quarter + t * (units - self.quarter) // 3) for t in range(4)]
        self.cuts = [0] + self.cuts
        self.g = self.grad_rows // PACK
        self.c = max(self.cuts[t + 1] - self.cuts[t] for t in range(4))
        self.count = tokens * nb * ns
        self.owned = width // ns

    def pack_grad(self, part):
        parts = [part[:, :LANES]]
        for column, lanes, _, rows in self.folds:
            piece = part[:, column:column + lanes]
            groups = -(-self.block // rows)
            short = groups * rows - self.block
            if short:
                piece = jnp.concatenate([piece, jnp.zeros((short, lanes), F32)], 0)
            row = [piece[i * rows:(i + 1) * rows] for i in range(groups)]
            if groups * lanes < LANES:
                row.append(jnp.zeros((rows, LANES - groups * lanes), F32))
            parts.append(jnp.concatenate(row, 1))
        stacked = jnp.concatenate(parts, 0)
        left = self.grad_rows - stacked.shape[0]
        if left:
            stacked = jnp.concatenate([stacked, jnp.zeros((left, LANES), F32)], 0)
        return stacked.reshape(self.g, PACK, LANES)

    def unpack_grad(self, packed):
        stacked = packed.reshape(self.grad_rows, LANES)
        parts = [stacked[:self.block]]
        for _, lanes, base, rows in self.folds:
            folded = stacked[base:base + rows]
            groups = -(-self.block // rows)
            piece = jnp.concatenate(
                [folded[:, i * lanes:(i + 1) * lanes] for i in range(groups)], 0)
            parts.append(piece[:self.block])
        return jnp.concatenate(parts, 1)

    def pack_cov(self, matrix):
        corner = matrix[LANES:, LANES:]
        corner = jnp.concatenate([corner, jnp.zeros((self.corner, LANES - self.corner), F32)], 1)
        stacked = jnp.concatenate([matrix[:, :LANES], corner], 0)
        left = self.cov_total - stacked.shape[0]
        if left:
            stacked = jnp.concatenate([stacked, jnp.zeros((left, LANES), F32)], 0)
        return stacked.reshape(self.cov_total // PACK, PACK, LANES)


def place(plan):
    batch = lax.axis_index("batch")
    seq = lax.axis_index("seq")
    core = batch % 2
    xy = (batch // 2 % 2) * 2 + seq % 2
    owner_block = seq // (plan.ns // plan.blocks)
    return seq, core, xy, owner_block


def putter(core, keep_ref, send_ref):
    def put(owner_core, at, value):
        @pl.when(core == owner_core)
        def _():
            keep_ref[at] = value.astype(keep_ref.dtype)

        @pl.when(core != owner_core)
        def _():
            send_ref[at] = value.astype(BF16)

    return put


def grad_kernel(plan, x_ref, y_ref, keep_ref, send_ref, turned_ref, x_own, y_own, sems):
    _, core, xy, owner_block = place(plan)
    copies = [
        pltpu.make_async_copy(x_ref, x_own, sems.at[0]),
        pltpu.make_async_copy(y_ref, y_own, sems.at[1]),
    ]
    for copy in copies:
        copy.start()
    put = putter(core, keep_ref, send_ref)
    copies[0].wait()
    turned = x_own[...].T
    turned_ref[...] = turned
    copies[1].wait()
    for column in range(plan.blocks):
        part = y_own[:, column * plan.block:(column + 1) * plan.block]
        grad = dot(turned, part, NN)
        slot = column % 2 ^ owner_block % 2
        for b in range(plan.blocks):
            packed = plan.pack_grad(grad[b * plan.block:(b + 1) * plan.block])
            put(b // 2, ((b % 2 * 2 + column // 2) ^ xy, slot), packed)


def cov_kernel(plan, x_ref, y_ref, turned_ref, keep_ref, send_ref):
    _, core, xy, owner_block = place(plan)
    put = putter(core, keep_ref, send_ref)
    block = plan.block
    for factor, ref in ((0, x_ref), (1, y_ref)):
        turned = turned_ref[...] if factor == 0 else ref[...].T
        for b in range(plan.blocks):
            part = ref[:, b * block:(b + 1) * block]
            stacked = plan.pack_cov(dot(turned[b * block:(b + 1) * block], part, NN))
            slot = (b ^ owner_block) * plan.c
            for t in range(4):
                piece = stacked[plan.cuts[t]:plan.cuts[t + 1]]
                put(factor, (t ^ xy, pl.ds(slot, piece.shape[0])), piece)


def split_kernel(keep_ref, recv_ref, after_ref, own_ref, *send_refs):
    own_ref[...] = keep_ref[0] + recv_ref[0].astype(F32)
    for j in range(1, 4):
        send_refs[j - 1][...] = (keep_ref[j] + recv_ref[j].astype(F32)).astype(BF16)


def total(parts, at):
    value = parts[0][at].astype(F32)
    for ref in parts[1:]:
        value = value + ref[at].astype(F32)
    return value


def sum_kernel(*refs):
    refs[-1][...] = total(refs[:-1], ...).astype(refs[-1].dtype)


def first_kernel(parts, outs):
    send_ref, keep_ref = outs
    keep_ref[...] = total(parts[:-1], 0)
    send_ref[...] = total(parts[:-1], 1).astype(BF16)


def second_kernel(plan, parts, outs):
    mine_ref, recv_ref, *cov_refs = parts
    send_ref, cov_ref = outs
    g, c = plan.g, plan.c
    send_ref[pl.ds(0, g)] = (mine_ref[...] + recv_ref[...].astype(F32)).astype(BF16)
    cov_ref[...] = total(cov_refs, pl.ds(0, 2 * c))
    send_ref[pl.ds(g, 2 * c)] = total(cov_refs, pl.ds(2 * c, 2 * c)).astype(BF16)


def split_two(value):
    high = value.astype(BF16)
    return high, (value - high.astype(F32)).astype(BF16)


def dot_split(a, b, dims):
    a_high, a_low = split_two(a)
    b_high, b_low = split_two(b)
    return dot(a_high, b_high, dims) + (dot(a_high, b_low, dims) + dot(a_low, b_high, dims))


def pick(ref, plan, wanted):
    value = ref[:, :plan.block]
    for n in range(1, plan.blocks):
        value = jnp.where(wanted == n, ref[:, n * plan.block:(n + 1) * plan.block], value)
    return value


def finish_kernel(plan, mine_ref, recv_ref, cov_ref, p_ref, q_ref, out_ref, keep_ref):
    _, core, xy, owner_block = place(plan)
    g, c = plan.g, plan.c
    keep_ref[...] = cov_ref[pl.ds(0, c)] + recv_ref[pl.ds(g, c)].astype(F32)
    other = cov_ref[pl.ds(c, c)] + recv_ref[pl.ds(g + c, c)].astype(F32)
    out_ref[pl.ds(g, c)] = other.astype(BF16)
    grad = mine_ref[pl.ds(0, g)].astype(F32) + recv_ref[pl.ds(0, g)].astype(F32)
    grad = plan.unpack_grad(grad) * (1.0 / plan.count)
    p_turned = pick(p_ref, plan, core * 2 + xy // 2)
    q_turned = pick(q_ref, plan, xy % 2 * 2 + owner_block % 2)
    done = dot_split(dot_split(p_turned.T, grad, NN), q_turned, NT)
    out_ref[pl.ds(0, g)] = plan.pack_grad(done).astype(BF16)


def bundle_kernel(plan, mine_ref, recv_ref, cov_ref, out_ref):
    g, c = plan.g, plan.c
    out_ref[pl.ds(0, g)] = mine_ref[pl.ds(0, g)]
    out_ref[pl.ds(g, g)] = recv_ref[pl.ds(0, g)]
    out_ref[pl.ds(2 * g, c)] = (cov_ref[...] + recv_ref[pl.ds(g, c)].astype(F32)).astype(BF16)


def assemble_kernel(plan, *refs):
    bundles, (in_ref, out_ref, grad_ref, whole, covs, done, sems, out_sems) = refs[:8], refs[8:]
    seq, core, xy, owner_block = place(plan)
    g, c, block = plan.g, plan.c, plan.block
    copies = []
    for i in range(8):
        q = (core ^ (i // 4)) * 4 + (xy ^ (i % 4))
        for e in range(2):
            copies.append(pltpu.make_async_copy(
                bundles[i].at[pl.ds(e * g, g)], whole.at[q * 2 + (e ^ owner_block % 2)],
                sems.at[3 * i + e]))
        copies.append(pltpu.make_async_copy(
            bundles[i].at[pl.ds(2 * g, c)], covs.at[q], sems.at[3 * i + 2]))
    for copy in copies:
        copy.start()
    for copy in copies:
        copy.wait()
    writes = []
    for b in range(plan.blocks):
        row = [plan.unpack_grad(whole[4 * b + n].astype(F32)) for n in range(plan.blocks)]
        done[b] = jnp.concatenate(row, 1).astype(BF16)
        write = pltpu.make_async_copy(
            done.at[b], grad_ref.at[pl.ds(b * block, block)], out_sems.at[b])
        write.start()
        writes.append(write)
    first = (seq % (plan.ns // plan.blocks)) * plan.owned
    row = lax.broadcasted_iota(jnp.int32, (plan.owned, block), 0) + first
    column = lax.broadcasted_iota(jnp.int32, (plan.owned, block), 1)
    select = jnp.where(row == column, 1.0, 0.0).astype(BF16)
    r128 = lax.broadcasted_iota(jnp.int32, (LANES, LANES), 0)
    c128 = lax.broadcasted_iota(jnp.int32, (LANES, LANES), 1)
    eye = jnp.where(r128 == c128, 1.0, 0.0).astype(BF16)
    for factor, ref in ((0, in_ref), (1, out_ref)):
        pieces = [
            covs[factor * 4 + t, pl.ds(0, plan.cuts[t + 1] - plan.cuts[t])].astype(F32)
            for t in range(4)
        ]
        stacked = jnp.concatenate(pieces, 0).reshape(plan.cov_total, LANES)
        left = stacked[:block]
        corner = stacked[block:block + plan.corner, :plan.corner]
        top = dot(eye, left[LANES:].astype(BF16), NT)
        right = jnp.concatenate([top, corner], 0)
        both = jnp.concatenate([left, right], 1).astype(BF16)
        ref[...] = dot(both, select, NT) * (1.0 / plan.count)
    for write in writes:
        write.wait()


def call(kernel, shapes, args, scratch=(), hbm_in=0, hbm_out=()):
    vmem = pl.BlockSpec(memory_space=pltpu.VMEM)
    hbm = pl.BlockSpec(memory_space=pltpu.HBM)
    args = [
        pltpu.with_memory_space_constraint(a, pltpu.HBM) if i < hbm_in else a
        for i, a in enumerate(args)
    ]
    return pl.pallas_call(
        kernel,
        out_shape=[jax.ShapeDtypeStruct(s, d) for s, d in shapes],
        in_specs=[hbm if i < hbm_in else vmem for i in range(len(args))],
        out_specs=[hbm if i in hbm_out else vmem for i in range(len(shapes))],
        scratch_shapes=list(scratch),
        compiler_params=pltpu.CompilerParams(vmem_limit_bytes=VMEM_LIMIT),
    )(*args)


def solution(mesh):
    nb, ns = mesh.shape["batch"], mesh.shape["seq"]

    def swap(value, batch_bits, seq_bits):
        pairs = [
            (b * ns + s, (b ^ batch_bits) * ns + (s ^ seq_bits))
            for b in range(nb) for s in range(ns)
        ]
        return lax.ppermute(value, AXES, pairs)

    def shards(layer_inputs, output_grads, input_inverse, output_inverse):
        tokens, width = layer_inputs.shape
        plan = Plan(tokens, width, input_inverse.shape[1], nb, ns)
        g, c = plan.g, plan.c
        step = ns // plan.blocks
        extra = [(bit, 0) for bit in (4, 8, 16, 32, 64) if bit < nb]
        extra += [(0, bit) for bit in (2, 4, 8, 16, 32, 64) if bit < step]

        def bind(kernel):
            def bound(*refs):
                return kernel(plan, *refs)

            return bound

        def group(kernel, outs, *head):
            def bound(*refs):
                return kernel(*head, refs[:-outs], refs[-outs:])

            return bound

        def units(n, dtype, *lead):
            return (*lead, n, PACK, LANES), dtype

        def exchange_parts(keep, send, after, shape):
            own, *sends = call(
                split_kernel, [(shape, F32)] + [(shape, BF16)] * 3,
                (keep, swap(send, 1, 0), after))
            peers = [swap(sends[2], 2, 1), swap(sends[1], 2, 0), swap(sends[0], 0, 1)]
            return [own] + peers

        def widen(parts, shape):
            for batch_bit, seq_bit in extra:
                summed, = call(sum_kernel, [(shape, BF16)], parts)
                parts = [summed, swap(summed, batch_bit, seq_bit)]
            return parts

        tile = (PACK, LANES)
        keep, send, turned = call(
            bind(grad_kernel),
            [units(g, F32, 4, 2), units(g, BF16, 4, 2), ((width, tokens), BF16)],
            (layer_inputs, output_grads), hbm_in=2,
            scratch=[pltpu.VMEM((tokens, width), BF16)] * 2 + [pltpu.SemaphoreType.DMA((2,))])
        cov_keep, cov_send = call(
            bind(cov_kernel), [units(4 * c, F32, 4), units(4 * c, BF16, 4)],
            (layer_inputs, output_grads, turned))
        parts = exchange_parts(keep, send, cov_keep, (2, g, *tile))
        cov_parts = exchange_parts(cov_keep, cov_send, parts[0], (4 * c, *tile))
        send, keep = call(
            group(first_kernel, 2), [units(g, BF16), units(g, F32)],
            widen(parts, (2, g, *tile)) + [cov_parts[0]])
        send, cov = call(
            group(second_kernel, 2, plan), [units(g + 2 * c, BF16), units(2 * c, F32)],
            [keep, swap(send, 0, step)] + widen(cov_parts, (4 * c, *tile)))
        send, cov = call(
            bind(finish_kernel), [units(g + c, BF16), units(c, F32)],
            (send, swap(send, 0, 2 * step), cov, input_inverse.T, output_inverse.T))
        done, = call(
            bind(bundle_kernel), [units(2 * g + c, BF16)],
            (send, swap(send, 0, step), cov))
        mine = [done, swap(done, 0, 1), swap(done, 2, 0), swap(done, 2, 1)]
        theirs = [swap(value, 1, 0) for value in mine]
        in_factor, out_factor, grad = call(
            bind(assemble_kernel),
            [((plan.block, plan.owned), F32)] * 2 + [((width, width), BF16)],
            mine + theirs, hbm_out=(2,),
            scratch=[
                pltpu.VMEM(units(g, BF16, 16)[0], BF16), pltpu.VMEM(units(c, BF16, 8)[0], BF16),
                pltpu.VMEM((plan.blocks, plan.block, width), BF16),
                pltpu.SemaphoreType.DMA((24,)), pltpu.SemaphoreType.DMA((plan.blocks,))])
        return in_factor.T, out_factor.T, grad

    return jax.shard_map(
        shards,
        mesh=mesh,
        in_specs=(P(AXES, None), P(AXES, None), P(), P()),
        out_specs=(P("seq", None), P("seq", None), P()),
        check_vma=False,
    )
```

profile of v0, /device:TPU:0, one launch (start us, length us, event | category | flops | bytes accessed | tf_op | source)
XLA Modules:
  0.0 60.2 jit_solution(3298893149427308442)
XLA Ops:
  0.6 0.0 copy-start.1
  0.6 0.0 copy-start
  0.6 7.5 %shard_map.67 = (f32[4,2,20,16,128]{4,3,2,1,0:T(8,128)S(1)}, bf16[4,2,20,16,128]{4,3,2,1,0:T(8,128)(2,1)S(1)}, bf16[800,800]{1,0:T(8,128)(2,1)S(1)}) custom-call(bf16[800,800]{1,0:T(8,128)(2,1)} %refs_0_.3, bf16[800,800]{1,0:T(8,128)(2,1)} %refs_1_.3), custom_call_target="tpu_custom_call" | custom-call | tf_op jit(solution)/shard_map/pallas_call | solution.py:279
  8.2 0.6 collective-permute-start
  8.7 0.0 copy-done.1
  8.8 0.0 copy-done
  8.8 3.8 %shard_map.68 = (f32[4,20,16,128]{3,2,1,0:T(8,128)S(1)}, bf16[4,20,16,128]{3,2,1,0:T(8,128)(2,1)S(1)}) custom-call(bf16[800,800]{1,0:T(8,128)(2,1)S(1)} %copy-done, bf16[800,800]{1,0:T(8,128)(2,1)S(1)} %copy-done.1, bf16[800,800]{1,0:T(8,128)(2,1)S(1)} %get-tuple-element.27.refs_2_), custom_call_target="tpu_custom_call" | custom-call | tf_op jit(solution)/shard_map/pallas_call | solution.py:279
  12.5 0.1 collective-permute-start.4
  12.6 0.0 collective-permute-done.recv_ref
  12.6 0.1 shard_map.69
  12.7 4.0 %collective-permute-start.1 = (bf16[2,20,16,128]{3,2,1,0:T(8,128)(2,1)S(1)}, bf16[2,20,16,128]{3,2,1,0:T(8,128)(2,1)S(1)}, u32[]{:S(2)}, u32[]{:S(2)}) collective-permute-start(bf16[2,20,16,128]{3,2,1,0:T(8,128)(2,1)S(1)} %get-tuple-element.30), channel_id=1, source_target_pairs={{0,17},{1,16},{2,19},{3,18},{4,21},{5,20},{6,23},{7,22},{8,25},{9,... | collective-permute-start | bytes 491528 | tf_op jit(solution)/shard_map/ppermute | solution.py:297
  16.7 0.5 collective-permute-start.2
  17.2 0.1 collective-permute-start.3
  17.4 0.0 collective-permute-done.4.recv_ref
  17.4 0.0 copy-start.2
  17.4 0.0 copy-start.3
  17.4 0.1 shard_map.70
  17.4 2.9 %collective-permute-start.6 = (bf16[20,16,128]{2,1,0:T(8,128)(2,1)S(1)}, bf16[20,16,128]{2,1,0:T(8,128)(2,1)S(1)}, u32[]{:S(2)}, u32[]{:S(2)}) collective-permute-start(bf16[20,16,128]{2,1,0:T(8,128)(2,1)S(1)} %get-tuple-element.37), channel_id=1, source_target_pairs={{0,17},{1,16},{2,19},{3,18},{4,21},{5,20},{6,23},{7,22},{8,25},{9,... | collective-permute-start | bytes 245768 | tf_op jit(solution)/shard_map/ppermute | solution.py:297
  20.4 0.5 collective-permute-start.7
  20.9 0.9 %collective-permute-done.1.refs_1_ = bf16[2,20,16,128]{3,2,1,0:T(8,128)(2,1)S(1)} collective-permute-done((bf16[2,20,16,128]{3,2,1,0:T(8,128)(2,1)S(1)}, bf16[2,20,16,128]{3,2,1,0:T(8,128)(2,1)S(1)}, u32[]{:S(2)}, u32[]{:S(2)}) %collective-permute-start.1) | collective-permute-done | bytes 163872 | tf_op jit(solution)/shard_map/ppermute | solution.py:297
  21.8 2.0 %collective-permute-start.8 = (bf16[20,16,128]{2,1,0:T(8,128)(2,1)S(1)}, bf16[20,16,128]{2,1,0:T(8,128)(2,1)S(1)}, u32[]{:S(2)}, u32[]{:S(2)}) collective-permute-start(bf16[20,16,128]{2,1,0:T(8,128)(2,1)S(1)} %get-tuple-element.39), channel_id=1, source_target_pairs={{0,1},{1,0},{2,3},{3,2},{4,5},{5,4},{6,7},{7,6},{8,9},{9,8},{10,11... | collective-permute-start | bytes 245768 | tf_op jit(solution)/shard_map/ppermute | solution.py:297
  23.8 2.0 %collective-permute-done.2.refs_2_ = bf16[2,20,16,128]{3,2,1,0:T(8,128)(2,1)S(1)} collective-permute-done((bf16[2,20,16,128]{3,2,1,0:T(8,128)(2,1)S(1)}, bf16[2,20,16,128]{3,2,1,0:T(8,128)(2,1)S(1)}, u32[]{:S(2)}, u32[]{:S(2)}) %collective-permute-start.2) | collective-permute-done | bytes 163872 | tf_op jit(solution)/shard_map/ppermute | solution.py:297
  25.8 0.2 collective-permute-done.3.refs_3_
  26.1 0.1 shard_map.71
  26.2 1.6 %collective-permute-start.5 = (bf16[20,16,128]{2,1,0:T(8,128)(2,1)S(1)}, bf16[20,16,128]{2,1,0:T(8,128)(2,1)S(1)}, u32[]{:S(2)}, u32[]{:S(2)}) collective-permute-start(bf16[20,16,128]{2,1,0:T(8,128)(2,1)S(1)} %get-tuple-element.36), channel_id=1, source_target_pairs={{0,2},{1,3},{2,0},{3,1},{4,6},{5,7},{6,4},{7,5},{8,10},{9,11},{10,... | collective-permute-start | bytes 245768 | tf_op jit(solution)/shard_map/ppermute | solution.py:297
  27.8 0.0 collective-permute-done.6.refs_3_
  27.8 0.6 %collective-permute-done.7.refs_4_ = bf16[20,16,128]{2,1,0:T(8,128)(2,1)S(1)} collective-permute-done((bf16[20,16,128]{2,1,0:T(8,128)(2,1)S(1)}, bf16[20,16,128]{2,1,0:T(8,128)(2,1)S(1)}, u32[]{:S(2)}, u32[]{:S(2)}) %collective-permute-start.7) | collective-permute-done | bytes 81952 | tf_op jit(solution)/shard_map/ppermute | solution.py:297
  28.4 0.0 collective-permute-done.8.refs_5_
  28.4 2.2 %collective-permute-done.5.refs_1_ = bf16[20,16,128]{2,1,0:T(8,128)(2,1)S(1)} collective-permute-done((bf16[20,16,128]{2,1,0:T(8,128)(2,1)S(1)}, bf16[20,16,128]{2,1,0:T(8,128)(2,1)S(1)}, u32[]{:S(2)}, u32[]{:S(2)}) %collective-permute-start.5) | collective-permute-done | bytes 81952 | tf_op jit(solution)/shard_map/ppermute | solution.py:297
  30.7 0.1 shard_map.72
  30.7 2.7 %collective-permute-start.9 = (bf16[30,16,128]{2,1,0:T(8,128)(2,1)S(1)}, bf16[30,16,128]{2,1,0:T(8,128)(2,1)S(1)}, u32[]{:S(2)}, u32[]{:S(2)}) collective-permute-start(bf16[30,16,128]{2,1,0:T(8,128)(2,1)S(1)} %get-tuple-element.40.refs_0_), channel_id=1, source_target_pairs={{0,4},{1,5},{2,6},{3,7},{4,0},{5,1},{6,2},{7,3},{8,12},{9,13},{10,... | collective-permute-start | bytes 368648 | tf_op jit(solution)/shard_map/ppermute | solution.py:297
  33.4 4.5 %collective-permute-done.9.refs_1_ = bf16[30,16,128]{2,1,0:T(8,128)(2,1)S(1)} collective-permute-done((bf16[30,16,128]{2,1,0:T(8,128)(2,1)S(1)}, bf16[30,16,128]{2,1,0:T(8,128)(2,1)S(1)}, u32[]{:S(2)}, u32[]{:S(2)}) %collective-permute-start.9) | collective-permute-done | bytes 122912 | tf_op jit(solution)/shard_map/ppermute | solution.py:297
  37.9 0.0 copy-done.2
  37.9 0.0 copy-done.3
  37.9 1.2 %shard_map.73 = (bf16[25,16,128]{2,1,0:T(8,128)(2,1)S(1)}, f32[5,16,128]{2,1,0:T(8,128)S(1)}) custom-call(bf16[30,16,128]{2,1,0:T(8,128)(2,1)S(1)} %get-tuple-element.40.refs_0_, bf16[30,16,128]{2,1,0:T(8,128)(2,1)S(1)} %collective-permute-done.9.refs_1_, f32[10,16,128]{2,1,0:T(8,128)S(1)} %get-tuple-element.41.refs_2_, f32[200,800]{1,0:T(8,128)S(1)} %bitcast.4, ...), custom_call_target="tpu_custom_call" | custom-call | tf_op jit(solution)/shard_map/pallas_call | solution.py:279
  39.1 0.7 %collective-permute-start.10 = (bf16[25,16,128]{2,1,0:T(8,128)(2,1)S(1)}, bf16[25,16,128]{2,1,0:T(8,128)(2,1)S(1)}, u32[]{:S(2)}, u32[]{:S(2)}) collective-permute-start(bf16[25,16,128]{2,1,0:T(8,128)(2,1)S(1)} %get-tuple-element.42.refs_0_), channel_id=1, source_target_pairs={{0,2},{1,3},{2,0},{3,1},{4,6},{5,7},{6,4},{7,5},{8,10},{9,11},{10,... | collective-permute-start | bytes 307208 | tf_op jit(solution)/shard_map/ppermute | solution.py:297
  39.8 4.0 %collective-permute-done.10.refs_1_ = bf16[25,16,128]{2,1,0:T(8,128)(2,1)S(1)} collective-permute-done((bf16[25,16,128]{2,1,0:T(8,128)(2,1)S(1)}, bf16[25,16,128]{2,1,0:T(8,128)(2,1)S(1)}, u32[]{:S(2)}, u32[]{:S(2)}) %collective-permute-start.10) | collective-permute-done | bytes 102432 | tf_op jit(solution)/shard_map/ppermute | solution.py:297
  43.8 2.6 %collective-permute-start.13 = (bf16[45,16,128]{2,1,0:T(8,128)(2,1)S(1)}, bf16[45,16,128]{2,1,0:T(8,128)(2,1)S(1)}, u32[]{:S(2)}, u32[]{:S(2)}) collective-permute-start(bf16[45,16,128]{2,1,0:T(8,128)(2,1)S(1)} %shard_map.74.refs_0_), channel_id=1, source_target_pairs={{0,17},{1,16},{2,19},{3,18},{4,21},{5,20},{6,23},{7,22},{8,25},{9,... | collective-permute-start | bytes 552968 | tf_op jit(solution)/shard_map/ppermute | solution.py:297
  46.4 0.5 collective-permute-start.12
  46.9 0.4 collective-permute-start.11
  47.4 0.0 collective-permute-start.14
  47.4 2.9 %collective-permute-done.13.refs_3_ = bf16[45,16,128]{2,1,0:T(8,128)(2,1)S(1)} collective-permute-done((bf16[45,16,128]{2,1,0:T(8,128)(2,1)S(1)}, bf16[45,16,128]{2,1,0:T(8,128)(2,1)S(1)}, u32[]{:S(2)}, u32[]{:S(2)}) %collective-permute-start.13) | collective-permute-done | bytes 184352 | tf_op jit(solution)/shard_map/ppermute | solution.py:297
  50.3 0.0 collective-permute-start.17
  50.3 2.1 %collective-permute-done.12.refs_2_ = bf16[45,16,128]{2,1,0:T(8,128)(2,1)S(1)} collective-permute-done((bf16[45,16,128]{2,1,0:T(8,128)(2,1)S(1)}, bf16[45,16,128]{2,1,0:T(8,128)(2,1)S(1)}, u32[]{:S(2)}, u32[]{:S(2)}) %collective-permute-start.12) | collective-permute-done | bytes 184352 | tf_op jit(solution)/shard_map/ppermute | solution.py:297
  52.4 0.0 collective-permute-start.16
  52.4 0.0 collective-permute-done.11.refs_1_
  52.5 0.5 collective-permute-start.15
  52.9 0.0 collective-permute-done.14.refs_4_
  53.0 0.0 collective-permute-done.17.refs_7_
  53.0 0.9 %collective-permute-done.16.refs_6_ = bf16[45,16,128]{2,1,0:T(8,128)(2,1)S(1)} collective-permute-done((bf16[45,16,128]{2,1,0:T(8,128)(2,1)S(1)}, bf16[45,16,128]{2,1,0:T(8,128)(2,1)S(1)}, u32[]{:S(2)}, u32[]{:S(2)}) %collective-permute-start.16) | collective-permute-done | bytes 184352 | tf_op jit(solution)/shard_map/ppermute | solution.py:297
  53.9 0.3 collective-permute-done.15.refs_5_
  54.1 6.1 %shard_map.75 = (f32[200,100]{1,0:T(8,128)}, f32[200,100]{1,0:T(8,128)}, bf16[800,800]{1,0:T(8,128)(2,1)}) custom-call(bf16[45,16,128]{2,1,0:T(8,128)(2,1)S(1)} %shard_map.74.refs_0_, bf16[45,16,128]{2,1,0:T(8,128)(2,1)S(1)} %collective-permute-done.11.refs_1_, bf16[45,16,128]{2,1,0:T(8,128)(2,1)S(1)} %collective-permute-done.12.refs_2_, ...), custom_call_target="tpu_custom_call" | custom-call | tf_op jit(solution)/shard_map/pallas_call | solution.py:279
  (1 shorter events, 0.0 us)
Async XLA Ops:
  0.6 8.1 %copy-start.1 = (bf16[800,800]{1,0:T(8,128)(2,1)S(1)}, bf16[800,800]{1,0:T(8,128)(2,1)}, u32[]{:S(2)}) copy-start(bf16[800,800]{1,0:T(8,128)(2,1)} %refs_1_.3) | copy-start | bytes 3840004
  0.6 8.1 %copy-start = (bf16[800,800]{1,0:T(8,128)(2,1)S(1)}, bf16[800,800]{1,0:T(8,128)(2,1)}, u32[]{:S(2)}) copy-start(bf16[800,800]{1,0:T(8,128)(2,1)} %refs_0_.3) | copy-start | bytes 3840004
  8.2 4.4 %collective-permute-start = (bf16[4,2,20,16,128]{4,3,2,1,0:T(8,128)(2,1)S(1)}, bf16[4,2,20,16,128]{4,3,2,1,0:T(8,128)(2,1)S(1)}, u32[]{:S(2)}, u32[]{:S(2)}) collective-permute-start(bf16[4,2,20,16,128]{4,3,2,1,0:T(8,128)(2,1)S(1)} %get-tuple-element.26), channel_id=1, source_target_pairs={{0,8},{1,9},{2,10},{3,11},{4,12},{5,13},{6,14},{7,15},{8,0},{9,1},... | collective-permute-start | bytes 1966088 | tf_op jit(solution)/shard_map/ppermute | solution.py:297
  12.5 4.8 %collective-permute-start.4 = (bf16[4,20,16,128]{3,2,1,0:T(8,128)(2,1)S(1)}, bf16[4,20,16,128]{3,2,1,0:T(8,128)(2,1)S(1)}, u32[]{:S(2)}, u32[]{:S(2)}) collective-permute-start(bf16[4,20,16,128]{3,2,1,0:T(8,128)(2,1)S(1)} %get-tuple-element.33), channel_id=1, source_target_pairs={{0,8},{1,9},{2,10},{3,11},{4,12},{5,13},{6,14},{7,15},{8,0},{9,1},... | collective-permute-start | bytes 983048 | tf_op jit(solution)/shard_map/ppermute | solution.py:297
  12.7 9.0 %collective-permute-start.1 = (bf16[2,20,16,128]{3,2,1,0:T(8,128)(2,1)S(1)}, bf16[2,20,16,128]{3,2,1,0:T(8,128)(2,1)S(1)}, u32[]{:S(2)}, u32[]{:S(2)}) collective-permute-start(bf16[2,20,16,128]{3,2,1,0:T(8,128)(2,1)S(1)} %get-tuple-element.30), channel_id=1, source_target_pairs={{0,17},{1,16},{2,19},{3,18},{4,21},{5,20},{6,23},{7,22},{8,25},{9,... | collective-permute-start | bytes 491528 | tf_op jit(solution)/shard_map/ppermute | solution.py:297
  16.7 9.1 %collective-permute-start.2 = (bf16[2,20,16,128]{3,2,1,0:T(8,128)(2,1)S(1)}, bf16[2,20,16,128]{3,2,1,0:T(8,128)(2,1)S(1)}, u32[]{:S(2)}, u32[]{:S(2)}) collective-permute-start(bf16[2,20,16,128]{3,2,1,0:T(8,128)(2,1)S(1)} %get-tuple-element.31), channel_id=1, source_target_pairs={{0,16},{1,17},{2,18},{3,19},{4,20},{5,21},{6,22},{7,23},{8,24},{9,... | collective-permute-start | bytes 491528 | tf_op jit(solution)/shard_map/ppermute | solution.py:297
  17.2 8.8 %collective-permute-start.3 = (bf16[2,20,16,128]{3,2,1,0:T(8,128)(2,1)S(1)}, bf16[2,20,16,128]{3,2,1,0:T(8,128)(2,1)S(1)}, u32[]{:S(2)}, u32[]{:S(2)}) collective-permute-start(bf16[2,20,16,128]{3,2,1,0:T(8,128)(2,1)S(1)} %get-tuple-element.32), channel_id=1, source_target_pairs={{0,1},{1,0},{2,3},{3,2},{4,5},{5,4},{6,7},{7,6},{8,9},{9,8},{10,11... | collective-permute-start | bytes 491528 | tf_op jit(solution)/shard_map/ppermute | solution.py:297
  17.4 20.5 %copy-start.2 = (f32[800,200]{0,1:T(8,128)S(1)}, f32[800,200]{0,1:T(8,128)}, u32[]{:S(2)}) copy-start(f32[800,200]{0,1:T(8,128)} %param.6) | copy-start | bytes 1920004
  17.4 20.5 %copy-start.3 = (f32[800,200]{0,1:T(8,128)S(1)}, f32[800,200]{0,1:T(8,128)}, u32[]{:S(2)}) copy-start(f32[800,200]{0,1:T(8,128)} %param.7) | copy-start | bytes 1920004
  17.4 10.4 %collective-permute-start.6 = (bf16[20,16,128]{2,1,0:T(8,128)(2,1)S(1)}, bf16[20,16,128]{2,1,0:T(8,128)(2,1)S(1)}, u32[]{:S(2)}, u32[]{:S(2)}) collective-permute-start(bf16[20,16,128]{2,1,0:T(8,128)(2,1)S(1)} %get-tuple-element.37), channel_id=1, source_target_pairs={{0,17},{1,16},{2,19},{3,18},{4,21},{5,20},{6,23},{7,22},{8,25},{9,... | collective-permute-start | bytes 245768 | tf_op jit(solution)/shard_map/ppermute | solution.py:297
  20.4 8.1 %collective-permute-start.7 = (bf16[20,16,128]{2,1,0:T(8,128)(2,1)S(1)}, bf16[20,16,128]{2,1,0:T(8,128)(2,1)S(1)}, u32[]{:S(2)}, u32[]{:S(2)}) collective-permute-start(bf16[20,16,128]{2,1,0:T(8,128)(2,1)S(1)} %get-tuple-element.38), channel_id=1, source_target_pairs={{0,16},{1,17},{2,18},{3,19},{4,20},{5,21},{6,22},{7,23},{8,24},{9,... | collective-permute-start | bytes 245768 | tf_op jit(solution)/shard_map/ppermute | solution.py:297
  21.8 6.7 %collective-permute-start.8 = (bf16[20,16,128]{2,1,0:T(8,128)(2,1)S(1)}, bf16[20,16,128]{2,1,0:T(8,128)(2,1)S(1)}, u32[]{:S(2)}, u32[]{:S(2)}) collective-permute-start(bf16[20,16,128]{2,1,0:T(8,128)(2,1)S(1)} %get-tuple-element.39), channel_id=1, source_target_pairs={{0,1},{1,0},{2,3},{3,2},{4,5},{5,4},{6,7},{7,6},{8,9},{9,8},{10,11... | collective-permute-start | bytes 245768 | tf_op jit(solution)/shard_map/ppermute | solution.py:297
  26.2 4.5 %collective-permute-start.5 = (bf16[20,16,128]{2,1,0:T(8,128)(2,1)S(1)}, bf16[20,16,128]{2,1,0:T(8,128)(2,1)S(1)}, u32[]{:S(2)}, u32[]{:S(2)}) collective-permute-start(bf16[20,16,128]{2,1,0:T(8,128)(2,1)S(1)} %get-tuple-element.36), channel_id=1, source_target_pairs={{0,2},{1,3},{2,0},{3,1},{4,6},{5,7},{6,4},{7,5},{8,10},{9,11},{10,... | collective-permute-start | bytes 245768 | tf_op jit(solution)/shard_map/ppermute | solution.py:297
  30.7 7.2 %collective-permute-start.9 = (bf16[30,16,128]{2,1,0:T(8,128)(2,1)S(1)}, bf16[30,16,128]{2,1,0:T(8,128)(2,1)S(1)}, u32[]{:S(2)}, u32[]{:S(2)}) collective-permute-start(bf16[30,16,128]{2,1,0:T(8,128)(2,1)S(1)} %get-tuple-element.40.refs_0_), channel_id=1, source_target_pairs={{0,4},{1,5},{2,6},{3,7},{4,0},{5,1},{6,2},{7,3},{8,12},{9,13},{10,... | collective-permute-start | bytes 368648 | tf_op jit(solution)/shard_map/ppermute | solution.py:297
  39.1 4.7 %collective-permute-start.10 = (bf16[25,16,128]{2,1,0:T(8,128)(2,1)S(1)}, bf16[25,16,128]{2,1,0:T(8,128)(2,1)S(1)}, u32[]{:S(2)}, u32[]{:S(2)}) collective-permute-start(bf16[25,16,128]{2,1,0:T(8,128)(2,1)S(1)} %get-tuple-element.42.refs_0_), channel_id=1, source_target_pairs={{0,2},{1,3},{2,0},{3,1},{4,6},{5,7},{6,4},{7,5},{8,10},{9,11},{10,... | collective-permute-start | bytes 307208 | tf_op jit(solution)/shard_map/ppermute | solution.py:297
  43.8 6.5 %collective-permute-start.13 = (bf16[45,16,128]{2,1,0:T(8,128)(2,1)S(1)}, bf16[45,16,128]{2,1,0:T(8,128)(2,1)S(1)}, u32[]{:S(2)}, u32[]{:S(2)}) collective-permute-start(bf16[45,16,128]{2,1,0:T(8,128)(2,1)S(1)} %shard_map.74.refs_0_), channel_id=1, source_target_pairs={{0,17},{1,16},{2,19},{3,18},{4,21},{5,20},{6,23},{7,22},{8,25},{9,... | collective-permute-start | bytes 552968 | tf_op jit(solution)/shard_map/ppermute | solution.py:297
  46.4 6.0 %collective-permute-start.12 = (bf16[45,16,128]{2,1,0:T(8,128)(2,1)S(1)}, bf16[45,16,128]{2,1,0:T(8,128)(2,1)S(1)}, u32[]{:S(2)}, u32[]{:S(2)}) collective-permute-start(bf16[45,16,128]{2,1,0:T(8,128)(2,1)S(1)} %shard_map.74.refs_0_), channel_id=1, source_target_pairs={{0,16},{1,17},{2,18},{3,19},{4,20},{5,21},{6,22},{7,23},{8,24},{9,... | collective-permute-start | bytes 552968 | tf_op jit(solution)/shard_map/ppermute | solution.py:297
  46.9 5.5 %collective-permute-start.11 = (bf16[45,16,128]{2,1,0:T(8,128)(2,1)S(1)}, bf16[45,16,128]{2,1,0:T(8,128)(2,1)S(1)}, u32[]{:S(2)}, u32[]{:S(2)}) collective-permute-start(bf16[45,16,128]{2,1,0:T(8,128)(2,1)S(1)} %shard_map.74.refs_0_), channel_id=1, source_target_pairs={{0,1},{1,0},{2,3},{3,2},{4,5},{5,4},{6,7},{7,6},{8,9},{9,8},{10,11... | collective-permute-start | bytes 552968 | tf_op jit(solution)/shard_map/ppermute | solution.py:297
  47.4 5.6 %collective-permute-start.14 = (bf16[45,16,128]{2,1,0:T(8,128)(2,1)S(1)}, bf16[45,16,128]{2,1,0:T(8,128)(2,1)S(1)}, u32[]{:S(2)}, u32[]{:S(2)}) collective-permute-start(bf16[45,16,128]{2,1,0:T(8,128)(2,1)S(1)} %shard_map.74.refs_0_), channel_id=1, source_target_pairs={{0,8},{1,9},{2,10},{3,11},{4,12},{5,13},{6,14},{7,15},{8,0},{9,1},... | collective-permute-start | bytes 552968 | tf_op jit(solution)/shard_map/ppermute | solution.py:297
  50.3 2.6 %collective-permute-start.17 = (bf16[45,16,128]{2,1,0:T(8,128)(2,1)S(1)}, bf16[45,16,128]{2,1,0:T(8,128)(2,1)S(1)}, u32[]{:S(2)}, u32[]{:S(2)}) collective-permute-start(bf16[45,16,128]{2,1,0:T(8,128)(2,1)S(1)} %collective-permute-done.13.refs_3_), channel_id=1, source_target_pairs={{0,8},{1,9},{2,10},{3,11},{4,12},{5,13},{6,14},{7,15},{8,0},{9,1},... | collective-permute-start | bytes 552968 | tf_op jit(solution)/shard_map/ppermute | solution.py:297
  52.4 1.4 %collective-permute-start.16 = (bf16[45,16,128]{2,1,0:T(8,128)(2,1)S(1)}, bf16[45,16,128]{2,1,0:T(8,128)(2,1)S(1)}, u32[]{:S(2)}, u32[]{:S(2)}) collective-permute-start(bf16[45,16,128]{2,1,0:T(8,128)(2,1)S(1)} %collective-permute-done.12.refs_2_), channel_id=1, source_target_pairs={{0,8},{1,9},{2,10},{3,11},{4,12},{5,13},{6,14},{7,15},{8,0},{9,1},... | collective-permute-start | bytes 552968 | tf_op jit(solution)/shard_map/ppermute | solution.py:297
  52.5 1.6 %collective-permute-start.15 = (bf16[45,16,128]{2,1,0:T(8,128)(2,1)S(1)}, bf16[45,16,128]{2,1,0:T(8,128)(2,1)S(1)}, u32[]{:S(2)}, u32[]{:S(2)}) collective-permute-start(bf16[45,16,128]{2,1,0:T(8,128)(2,1)S(1)} %collective-permute-done.11.refs_1_), channel_id=1, source_target_pairs={{0,8},{1,9},{2,10},{3,11},{4,12},{5,13},{6,14},{7,15},{8,0},{9,1},... | collective-permute-start | bytes 552968 | tf_op jit(solution)/shard_map/ppermute | solution.py:297
where the time goes:
time: 60.3 us; the launch traced here: 60.2 us
  waiting for transfers between devices  20.8 us (34%)
  starting transfers between devices  19.8 us (33%)
  Pallas kernels  18.9 us (31%)
  between operations  0.71 us (1%)
    ppermute x18, waiting for transfers between devices, swap(): return lax.ppermute(value, AXES, pairs)  20.8 us
    ppermute x18, starting transfers between devices, swap(): return lax.ppermute(value, AXES, pairs)  19.8 us
    pallas_call x9, Pallas kernels, call(): pl.pallas_call(kernel, out_shape=[jax.ShapeDtypeStruct(s, d) for s, d in...  18.9 us
  transfers between devices with their start and end apart: 18, of which 11 were waited for; matrix products, arithmetic and copies ran while one was open for 0% of the time, Pallas kernels for 7%

commit v1 on v0

v1 whole, which is shorter than its diff:
```python
import jax
import jax.numpy as jnp
from jax import lax
from jax.experimental import pallas as pl
from jax.experimental.pallas import tpu as pltpu
from jax.sharding import PartitionSpec as P


AXES = ("batch", "seq")
LANES = 128
PACK = 16
VMEM_LIMIT = 16 << 20
F32 = jnp.float32
BF16 = jnp.bfloat16
NN = (((1,), (0,)), ((), ()))
NT = (((1,), (1,)), ((), ()))
TN = (((0,), (0,)), ((), ()))


def dot(a, b, dims):
    return lax.dot_general(a, b, dims, preferred_element_type=F32)


def turn(value, shift):
    shift %= LANES
    return pltpu.roll(value, shift, 1) if shift else value


def up(value, step):
    return -(-value // step) * step


class Plan:
    def __init__(self, tokens, width, block, nb, ns):
        self.tokens, self.width, self.block = tokens, width, block
        self.nb, self.ns = nb, ns
        self.blocks = width // block
        assert self.blocks == 4 and nb % 2 == 0 and nb >= 4 and ns >= 8
        assert LANES < block <= 2 * LANES and block % 8 == 0
        self.tiles = 2 * block // LANES
        self.tail = 2 * block - self.tiles * LANES
        assert 0 < 2 * self.tail <= LANES and LANES % self.tail == 0
        self.fold = LANES // self.tail
        self.fold_rows = up(-(-block // self.fold), 8)
        self.grad_rows = up(block * self.tiles + self.fold_rows, 2 * PACK)
        self.corner = block - LANES
        self.cov_total = up(block + self.corner, PACK)
        units = self.cov_total // PACK
        self.quarter = -(-units // 4)
        self.cuts = [min(units, self.quarter + t * (units - self.quarter) // 3) for t in range(4)]
        self.cuts = [0] + self.cuts
        self.g = self.grad_rows // PACK // 2
        self.c = max(self.cuts[t + 1] - self.cuts[t] for t in range(4))
        self.count = tokens * nb * ns
        self.owned = width // ns

    def lane(self):
        return lax.broadcasted_iota(jnp.int32, (self.block, LANES), 1)

    def pack_pair(self, tiles, h):
        if h == 0:
            sent, rest, start = list(tiles[:-1]), tiles[-1], 0
        else:
            mixed = jnp.where(self.lane() < self.tail, tiles[-1], tiles[0])
            sent, rest, start = [mixed] + list(tiles[1:-1]), tiles[-1], self.tail
        groups = -(-self.block // self.fold_rows)
        short = groups * self.fold_rows - self.block
        if short:
            rest = jnp.concatenate([rest, jnp.zeros((short, LANES), F32)], 0)
        lane = lax.broadcasted_iota(jnp.int32, (self.fold_rows, LANES), 1)
        folded = jnp.zeros((self.fold_rows, LANES), F32)
        for i in range(groups):
            piece = rest[i * self.fold_rows:(i + 1) * self.fold_rows]
            piece = turn(piece, i * self.tail - start)
            folded = jnp.where(lane // self.tail == i, piece, folded)
        stacked = jnp.concatenate(sent + [folded], 0)
        left = self.grad_rows - stacked.shape[0]
        if left:
            stacked = jnp.concatenate([stacked, jnp.zeros((left, LANES), F32)], 0)
        return stacked.reshape(2, self.g, PACK, LANES)

    def unpack_pair(self, packed, h):
        stacked = packed.reshape(self.grad_rows, LANES)
        sent = [stacked[k * self.block:(k + 1) * self.block] for k in range(self.tiles)]
        base = self.tiles * self.block
        folded = stacked[base:base + self.fold_rows]
        groups = -(-self.block // self.fold_rows)
        start = 0 if h == 0 else self.tail
        rest = jnp.concatenate(
            [turn(folded, start - i * self.tail) for i in range(groups)], 0)[:self.block]
        if h == 0:
            return sent + [rest]
        last = jnp.where(self.lane() < self.tail, sent[0], rest)
        return sent + [last]

    def tiles_of(self, rows, h):
        start = h * self.tiles * LANES
        stop = min(start + (self.tiles + 1) * LANES, self.width)
        tiles = [rows[:, at:min(at + LANES, stop)] for at in range(start, stop, LANES)]
        missing = LANES - tiles[-1].shape[1]
        if missing:
            pad = jnp.zeros((self.block, missing), F32)
            tiles[-1] = jnp.concatenate([tiles[-1], pad], 1)
        return tiles

    def pack_cov(self, matrix):
        corner = matrix[LANES:, LANES:]
        corner = jnp.concatenate([corner, jnp.zeros((self.corner, LANES - self.corner), F32)], 1)
        stacked = jnp.concatenate([matrix[:, :LANES], corner], 0)
        left = self.cov_total - stacked.shape[0]
        if left:
            stacked = jnp.concatenate([stacked, jnp.zeros((left, LANES), F32)], 0)
        return stacked.reshape(self.cov_total // PACK, PACK, LANES)


def place(plan):
    batch = lax.axis_index("batch")
    seq = lax.axis_index("seq")
    core = batch % 2
    xy = (batch // 2 % 2) * 2 + seq % 2
    owner_block = seq // (plan.ns // plan.blocks)
    return seq, core, xy, owner_block


def grad_kernel(plan, x_ref, y_ref, keep_ref, send_ref, both_ref, sems):
    _, core, xy, _ = place(plan)
    copies = [
        pltpu.make_async_copy(x_ref, both_ref.at[0], sems.at[0]),
        pltpu.make_async_copy(y_ref, both_ref.at[1], sems.at[1]),
    ]
    for copy in copies:
        copy.start()
    copies[0].wait()
    turned = both_ref[0].T
    copies[1].wait()
    grad = dot(turned, both_ref[1], NN)
    for b in range(plan.blocks):
        rows = grad[b * plan.block:(b + 1) * plan.block]
        for h in range(2):
            packed = plan.pack_pair(plan.tiles_of(rows, h), h)
            j = (b % 2 * 2 + h) ^ xy

            @pl.when(core == b // 2)
            def _():
                keep_ref[j] = packed

            @pl.when(core != b // 2)
            def _():
                send_ref[j] = packed.astype(BF16)


def cov_kernel(plan, mine, both_ref, after_ref, out_ref):
    _, core, xy, owner_block = place(plan)
    block = plan.block
    factor = core if mine else 1 - core
    for b in range(plan.blocks):
        part = both_ref[factor, :, b * block:(b + 1) * block]
        stacked = plan.pack_cov(dot(part, part, TN))
        slot = (b ^ owner_block) * plan.c
        for t in range(4):
            piece = stacked[plan.cuts[t]:plan.cuts[t + 1]]
            out_ref[t ^ xy, pl.ds(slot, piece.shape[0])] = piece.astype(out_ref.dtype)


def split_kernel(keep_ref, recv_ref, after_ref, own_ref, *send_refs):
    own_ref[...] = keep_ref[0] + recv_ref[0].astype(F32)
    for j in range(1, 4):
        send_refs[j - 1][...] = (keep_ref[j] + recv_ref[j].astype(F32)).astype(BF16)


def total(parts, at):
    value = parts[0][at].astype(F32)
    for ref in parts[1:]:
        value = value + ref[at].astype(F32)
    return value


def sum_kernel(*refs):
    refs[-1][...] = total(refs[:-1], ...).astype(refs[-1].dtype)


def first_kernel(plan, parts, outs):
    send_ref, keep_ref = outs
    half = place(plan)[3] % 2
    keep_ref[...] = total(parts[:-1], half)
    send_ref[...] = total(parts[:-1], 1 - half).astype(BF16)


def second_kernel(plan, parts, outs):
    mine_ref, recv_ref, *cov_refs = parts
    send_ref, cov_ref = outs
    g, c = plan.g, plan.c
    send_ref[pl.ds(0, g)] = (mine_ref[...] + recv_ref[...].astype(F32)).astype(BF16)
    cov_ref[...] = total(cov_refs, pl.ds(0, 2 * c))
    send_ref[pl.ds(g, 2 * c)] = total(cov_refs, pl.ds(2 * c, 2 * c)).astype(BF16)


def third_kernel(plan, mine_ref, recv_ref, cov_ref, out_ref, keep_ref):
    g, c = plan.g, plan.c
    out_ref[pl.ds(0, g)] = total((mine_ref, recv_ref), pl.ds(0, g)).astype(BF16)
    other = cov_ref[pl.ds(c, c)] + recv_ref[pl.ds(g + c, c)].astype(F32)
    out_ref[pl.ds(g, c)] = other.astype(BF16)
    keep_ref[...] = cov_ref[pl.ds(0, c)] + recv_ref[pl.ds(g, c)].astype(F32)


def split_two(value):
    high = value.astype(BF16)
    return high, (value - high.astype(F32)).astype(BF16)


def dot_split(a, b, dims):
    a_high, a_low = split_two(a)
    b_high, b_low = split_two(b)
    return dot(a_high, b_high, dims) + (dot(a_high, b_low, dims) + dot(a_low, b_high, dims))


def pick(ref, plan, wanted):
    value = ref[:, :plan.block]
    for n in range(1, plan.blocks):
        value = jnp.where(wanted == n, ref[:, n * plan.block:(n + 1) * plan.block], value)
    return value


def finish_kernel(plan, mine_ref, recv_ref, cov_ref, p_ref, q_ref, out_ref, whole):
    _, core, xy, owner_block = place(plan)
    g, c, block = plan.g, plan.c, plan.block
    cov = cov_ref[...] + recv_ref[pl.ds(g, c)].astype(F32)
    out_ref[pl.ds(2 * g, c)] = cov.astype(BF16)
    whole[owner_block % 2] = mine_ref[pl.ds(0, g)].astype(F32)
    whole[1 - owner_block % 2] = recv_ref[pl.ds(0, g)].astype(F32)
    low = xy % 2 == 0
    pair = whole[...]
    natural = [jnp.concatenate(plan.unpack_pair(pair, h), 1).astype(BF16) for h in range(2)]
    p_high, p_low = split_two(pick(p_ref, plan, core * 2 + xy // 2).T)
    done = []
    for e in range(2):
        at = e * block
        part = jnp.where(low, natural[0][:, at:at + block].astype(F32),
                         natural[1][:, at + plan.tail:at + plan.tail + block].astype(F32))
        part = part.astype(BF16)
        left = dot(p_high, part, NN) + dot(p_low, part, NN)
        done.append(dot_split(left, pick(q_ref, plan, xy % 2 * 2 + e), NT) * (1.0 / plan.count))
    tail = jnp.zeros((block, plan.tail), F32)
    end = jnp.zeros((block, LANES - 2 * plan.tail), F32)
    packed = []
    for h, order in ((0, done + [tail, end]), (1, [tail] + done + [end])):
        row = jnp.concatenate(order, 1)
        tiles = [row[:, k * LANES:(k + 1) * LANES] for k in range(plan.tiles + 1)]
        packed.append(plan.pack_pair(tiles, h))
    packed = jnp.where(low, packed[0], packed[1]).astype(BF16)
    out_ref[pl.ds(0, 2 * g)] = packed.reshape(2 * g, PACK, LANES)


def assemble_kernel(plan, *refs):
    bundles, (in_ref, out_ref, grad_ref, whole, done, sems, out_sems) = refs[:8], refs[8:]
    seq, core, xy, _ = place(plan)
    g, block = plan.g, plan.block
    copies = []
    for i in range(8):
        q = (core ^ (i // 4)) * 4 + (xy ^ (i % 4))
        copies.append(pltpu.make_async_copy(bundles[i], whole.at[q], sems.at[i]))
    for copy in copies:
        copy.start()
    for copy in copies:
        copy.wait()
    writes = []
    for b in range(plan.blocks):
        low, high = (
            plan.unpack_pair(whole[2 * b + h, pl.ds(0, 2 * g)].astype(F32), h) for h in range(2))
        middle = jnp.where(plan.lane() < plan.tail, low[-1], high[0])
        row = low[:-1] + [middle] + high[1:-1] + [high[-1][:, :2 * plan.tail]]
        done[b] = jnp.concatenate(row, 1).astype(BF16)
        write = pltpu.make_async_copy(
            done.at[b], grad_ref.at[pl.ds(b * block, block)], out_sems.at[b])
        write.start()
        writes.append(write)
    first = (seq % (plan.ns // plan.blocks)) * plan.owned
    row = lax.broadcasted_iota(jnp.int32, (plan.owned, block), 0) + first
    column = lax.broadcasted_iota(jnp.int32, (plan.owned, block), 1)
    select = jnp.where(row == column, 1.0, 0.0).astype(BF16)
    r128 = lax.broadcasted_iota(jnp.int32, (LANES, LANES), 0)
    c128 = lax.broadcasted_iota(jnp.int32, (LANES, LANES), 1)
    eye = jnp.where(r128 == c128, 1.0, 0.0).astype(BF16)
    for factor, ref in ((0, in_ref), (1, out_ref)):
        pieces = [
            whole[factor * 4 + t, pl.ds(2 * g, plan.cuts[t + 1] - plan.cuts[t])].astype(F32)
            for t in range(4)
        ]
        stacked = jnp.concatenate(pieces, 0).reshape(plan.cov_total, LANES)
        left = stacked[:block]
        corner = stacked[block:block + plan.corner, :plan.corner]
        top = dot(eye, left[LANES:].astype(BF16), NT)
        right = jnp.concatenate([top, corner], 0)
        both = jnp.concatenate([left, right], 1).astype(BF16)
        ref[...] = dot(both, select, NT) * (1.0 / plan.count)
    for write in writes:
        write.wait()


def call(kernel, shapes, args, scratch=(), hbm_in=0, hbm_out=()):
    vmem = pl.BlockSpec(memory_space=pltpu.VMEM)
    hbm = pl.BlockSpec(memory_space=pltpu.HBM)
    args = [
        pltpu.with_memory_space_constraint(a, pltpu.HBM) if i < hbm_in else a
        for i, a in enumerate(args)
    ]
    return pl.pallas_call(
        kernel,
        out_shape=[jax.ShapeDtypeStruct(s, d) for s, d in shapes],
        in_specs=[hbm if i < hbm_in else vmem for i in range(len(args))],
        out_specs=[hbm if i in hbm_out else vmem for i in range(len(shapes))],
        scratch_shapes=list(scratch),
        compiler_params=pltpu.CompilerParams(vmem_limit_bytes=VMEM_LIMIT),
    )(*args)


def solution(mesh):
    nb, ns = mesh.shape["batch"], mesh.shape["seq"]

    def swap(value, batch_bits, seq_bits):
        pairs = [
            (b * ns + s, (b ^ batch_bits) * ns + (s ^ seq_bits))
            for b in range(nb) for s in range(ns)
        ]
        return lax.ppermute(value, AXES, pairs)

    def shards(layer_inputs, output_grads, input_inverse, output_inverse):
        tokens, width = layer_inputs.shape
        plan = Plan(tokens, width, input_inverse.shape[1], nb, ns)
        g, c = plan.g, plan.c
        step = ns // plan.blocks
        extra = [(bit, 0) for bit in (4, 8, 16, 32, 64) if bit < nb]
        extra += [(0, bit) for bit in (2, 4, 8, 16, 32, 64) if bit < step]

        def bind(kernel):
            def bound(*refs):
                return kernel(plan, *refs)

            return bound

        def group(kernel, outs, *head):
            def bound(*refs):
                return kernel(*head, refs[:-outs], refs[-outs:])

            return bound

        def units(n, dtype, *lead):
            return (*lead, n, PACK, LANES), dtype

        def exchange_parts(keep, send, after, shape):
            own, *sends = call(
                split_kernel, [(shape, F32)] + [(shape, BF16)] * 3,
                (keep, swap(send, 1, 0), after))
            peers = [swap(sends[2], 2, 1), swap(sends[1], 2, 0), swap(sends[0], 0, 1)]
            return [own] + peers

        def widen(parts, shape):
            for batch_bit, seq_bit in extra:
                summed, = call(sum_kernel, [(shape, BF16)], parts)
                parts = [summed, swap(summed, batch_bit, seq_bit)]
            return parts

        tile = (PACK, LANES)
        keep, send, both = call(
            bind(grad_kernel),
            [units(g, F32, 4, 2), units(g, BF16, 4, 2), ((2, tokens, width), BF16)],
            (layer_inputs, output_grads), hbm_in=2,
            scratch=[pltpu.SemaphoreType.DMA((2,))])
        cov_send, = call(
            group(lambda refs, outs: cov_kernel(plan, False, *refs, *outs), 1),
            [units(4 * c, BF16, 4)], (both, send))
        parts = exchange_parts(keep, send, cov_send, (2, g, *tile))
        cov_keep, = call(
            group(lambda refs, outs: cov_kernel(plan, True, *refs, *outs), 1),
            [units(4 * c, F32, 4)], (both, parts[0]))
        cov_parts = exchange_parts(cov_keep, cov_send, parts[0], (4 * c, *tile))
        send, keep = call(
            group(first_kernel, 2, plan), [units(g, BF16), units(g, F32)],
            widen(parts, (2, g, *tile)) + [cov_parts[0]])
        send, cov = call(
            group(second_kernel, 2, plan), [units(g + 2 * c, BF16), units(2 * c, F32)],
            [keep, swap(send, 0, step)] + widen(cov_parts, (4 * c, *tile)))
        send, cov = call(
            bind(third_kernel), [units(g + c, BF16), units(c, F32)],
            (send, swap(send, 0, 2 * step), cov))
        done, = call(
            bind(finish_kernel), [units(2 * g + c, BF16)],
            (send, swap(send, 0, step), cov, input_inverse.T, output_inverse.T),
            scratch=[pltpu.VMEM(units(g, F32, 2)[0], F32)])
        mine = [done, swap(done, 0, 1), swap(done, 2, 0), swap(done, 2, 1)]
        theirs = [swap(value, 1, 0) for value in mine]
        in_factor, out_factor, grad = call(
            bind(assemble_kernel),
            [((plan.block, plan.owned), F32)] * 2 + [((width, width), BF16)],
            mine + theirs, hbm_out=(2,),
            scratch=[
                pltpu.VMEM(units(2 * g + c, BF16, 8)[0], BF16),
                pltpu.VMEM((plan.blocks, plan.block, width), BF16),
                pltpu.SemaphoreType.DMA((8,)), pltpu.SemaphoreType.DMA((plan.blocks,))])
        return in_factor.T, out_factor.T, grad

    return jax.shard_map(
        shards,
        mesh=mesh,
        in_specs=(P(AXES, None), P(AXES, None), P(), P()),
        out_specs=(P("seq", None), P("seq", None), P()),
        check_vma=False,
    )
```

time: 60.3 us -> 54.1 us (0.90)
  Pallas kernels: 18.9 us -> 13.1 us
    pallas_call x9 -> x10, Pallas kernels: 18.9 us -> 13.1 us  [call(): pl.pallas_call(kernel, out_shape=[jax.ShapeDtypeStruct(s, d) for s, d in...]
  transfers between devices with their start and end apart: 18 -> 18, of which waited for: 11 -> 10; matrix products, arithmetic and copies ran while one was open for 0% -> 0% of each run, Pallas kernels for 7% -> 5%
where the time goes in v1:
time: 54.1 us; the launch traced here: 53.9 us
  waiting for transfers between devices  20.8 us (38%)
  starting transfers between devices  19.2 us (35%)
  Pallas kernels  13.1 us (24%)
  between operations  0.73 us (1%)
    ppermute x18, waiting for transfers between devices, swap(): return lax.ppermute(value, AXES, pairs)  20.8 us
    ppermute x18, starting transfers between devices, swap(): return lax.ppermute(value, AXES, pairs)  19.2 us
    pallas_call x10, Pallas kernels, call(): pl.pallas_call(kernel, out_shape=[jax.ShapeDtypeStruct(s, d) for s, d in...  13.1 us
  transfers between devices with their start and end apart: 18, of which 10 were waited for; matrix products, arithmetic and copies ran while one was open for 0% of the time, Pallas kernels for 5%

profile of v1, /device:TPU:0, one launch (start us, length us, event | category | flops | bytes accessed | tf_op | source)
XLA Modules:
  0.0 53.9 jit_solution(1627400708820847521)
XLA Ops:
  0.6 4.3 %shard_map.67 = (f32[4,2,20,16,128]{4,3,2,1,0:T(8,128)S(1)}, bf16[4,2,20,16,128]{4,3,2,1,0:T(8,128)(2,1)S(1)}, bf16[2,800,800]{2,1,0:T(8,128)(2,1)S(1)}) custom-call(bf16[800,800]{1,0:T(8,128)(2,1)} %refs_0_.1, bf16[800,800]{1,0:T(8,128)(2,1)} %refs_1_.1), custom_call_target="tpu_custom_call" | custom-call | tf_op jit(solution)/shard_map/pallas_call | solution.py:307
  5.0 0.5 %collective-permute-start = (bf16[4,2,20,16,128]{4,3,2,1,0:T(8,128)(2,1)S(1)}, bf16[4,2,20,16,128]{4,3,2,1,0:T(8,128)(2,1)S(1)}, u32[]{:S(2)}, u32[]{:S(2)}) collective-permute-start(bf16[4,2,20,16,128]{4,3,2,1,0:T(8,128)(2,1)S(1)} %get-tuple-element.24.refs_1_), channel_id=1, source_target_pairs={{0,8},{1,9},{2,10},{3,11},{4,12},{5,13},{6,14},{7,15},{8,0},{9,1},... | collective-permute-start | bytes 1966088 | tf_op jit(solution)/shard_map/ppermute | solution.py:325
  5.5 1.4 %shard_map.68.after_ref = bf16[4,20,16,128]{3,2,1,0:T(8,128)(2,1)S(1)} custom-call(bf16[2,800,800]{2,1,0:T(8,128)(2,1)S(1)} %get-tuple-element.25.refs_0_, bf16[4,2,20,16,128]{4,3,2,1,0:T(8,128)(2,1)S(1)} %get-tuple-element.24.refs_1_), custom_call_target="tpu_custom_call" | custom-call | tf_op jit(solution)/shard_map/pallas_call | solution.py:307
  6.9 0.1 collective-permute-start.4
  7.0 0.3 collective-permute-done.recv_ref
  7.3 0.1 shard_map.69
  7.4 3.9 %collective-permute-start.1 = (bf16[2,20,16,128]{3,2,1,0:T(8,128)(2,1)S(1)}, bf16[2,20,16,128]{3,2,1,0:T(8,128)(2,1)S(1)}, u32[]{:S(2)}, u32[]{:S(2)}) collective-permute-start(bf16[2,20,16,128]{3,2,1,0:T(8,128)(2,1)S(1)} %get-tuple-element.27), channel_id=1, source_target_pairs={{0,17},{1,16},{2,19},{3,18},{4,21},{5,20},{6,23},{7,22},{8,25},{9,... | collective-permute-start | bytes 491528 | tf_op jit(solution)/shard_map/ppermute | solution.py:325
  11.3 0.5 collective-permute-start.2
  11.8 0.1 collective-permute-start.3
  11.9 1.4 %shard_map.70.keep_ref = f32[4,20,16,128]{3,2,1,0:T(8,128)S(1)} custom-call(bf16[2,800,800]{2,1,0:T(8,128)(2,1)S(1)} %get-tuple-element.25.refs_0_, f32[2,20,16,128]{3,2,1,0:T(8,128)S(1)} %get-tuple-element.26.refs_1_.after_ref.refs_0_), custom_call_target="tpu_custom_call" | custom-call | tf_op jit(solution)/shard_map/pallas_call | solution.py:307
  13.3 0.0 copy-start
  13.3 0.0 copy-start.1
  13.3 0.0 collective-permute-done.4.recv_ref
  13.3 0.1 shard_map.71
  13.4 2.9 %collective-permute-start.6 = (bf16[20,16,128]{2,1,0:T(8,128)(2,1)S(1)}, bf16[20,16,128]{2,1,0:T(8,128)(2,1)S(1)}, u32[]{:S(2)}, u32[]{:S(2)}) collective-permute-start(bf16[20,16,128]{2,1,0:T(8,128)(2,1)S(1)} %get-tuple-element.33), channel_id=1, source_target_pairs={{0,17},{1,16},{2,19},{3,18},{4,21},{5,20},{6,23},{7,22},{8,25},{9,... | collective-permute-start | bytes 245768 | tf_op jit(solution)/shard_map/ppermute | solution.py:325
  16.3 0.5 collective-permute-start.7
  16.8 0.0 collective-permute-done.1.refs_1_
  16.8 1.5 %collective-permute-start.8 = (bf16[20,16,128]{2,1,0:T(8,128)(2,1)S(1)}, bf16[20,16,128]{2,1,0:T(8,128)(2,1)S(1)}, u32[]{:S(2)}, u32[]{:S(2)}) collective-permute-start(bf16[20,16,128]{2,1,0:T(8,128)(2,1)S(1)} %get-tuple-element.35), channel_id=1, source_target_pairs={{0,1},{1,0},{2,3},{3,2},{4,5},{5,4},{6,7},{7,6},{8,9},{9,8},{10,11... | collective-permute-start | bytes 245768 | tf_op jit(solution)/shard_map/ppermute | solution.py:325
  18.3 2.0 %collective-permute-done.2.refs_2_ = bf16[2,20,16,128]{3,2,1,0:T(8,128)(2,1)S(1)} collective-permute-done((bf16[2,20,16,128]{3,2,1,0:T(8,128)(2,1)S(1)}, bf16[2,20,16,128]{3,2,1,0:T(8,128)(2,1)S(1)}, u32[]{:S(2)}, u32[]{:S(2)}) %collective-permute-start.2) | collective-permute-done | bytes 163872 | tf_op jit(solution)/shard_map/ppermute | solution.py:325
  20.4 0.0 collective-permute-done.3.refs_3_
  20.4 0.1 shard_map.72
  20.5 1.9 %collective-permute-start.5 = (bf16[20,16,128]{2,1,0:T(8,128)(2,1)S(1)}, bf16[20,16,128]{2,1,0:T(8,128)(2,1)S(1)}, u32[]{:S(2)}, u32[]{:S(2)}) collective-permute-start(bf16[20,16,128]{2,1,0:T(8,128)(2,1)S(1)} %get-tuple-element.32), channel_id=1, source_target_pairs={{0,2},{1,3},{2,0},{3,1},{4,6},{5,7},{6,4},{7,5},{8,10},{9,11},{10,... | collective-permute-start | bytes 245768 | tf_op jit(solution)/shard_map/ppermute | solution.py:325
  22.3 0.0 collective-permute-done.6.refs_3_
  22.3 0.7 %collective-permute-done.7.refs_4_ = bf16[20,16,128]{2,1,0:T(8,128)(2,1)S(1)} collective-permute-done((bf16[20,16,128]{2,1,0:T(8,128)(2,1)S(1)}, bf16[20,16,128]{2,1,0:T(8,128)(2,1)S(1)}, u32[]{:S(2)}, u32[]{:S(2)}) %collective-permute-start.7) | collective-permute-done | bytes 81952 | tf_op jit(solution)/shard_map/ppermute | solution.py:325
  23.1 0.0 collective-permute-done.8.refs_5_
  23.1 1.9 %collective-permute-done.5.refs_1_ = bf16[20,16,128]{2,1,0:T(8,128)(2,1)S(1)} collective-permute-done((bf16[20,16,128]{2,1,0:T(8,128)(2,1)S(1)}, bf16[20,16,128]{2,1,0:T(8,128)(2,1)S(1)}, u32[]{:S(2)}, u32[]{:S(2)}) %collective-permute-start.5) | collective-permute-done | bytes 81952 | tf_op jit(solution)/shard_map/ppermute | solution.py:325
  25.0 0.1 shard_map.73
  25.0 2.9 %collective-permute-start.9 = (bf16[30,16,128]{2,1,0:T(8,128)(2,1)S(1)}, bf16[30,16,128]{2,1,0:T(8,128)(2,1)S(1)}, u32[]{:S(2)}, u32[]{:S(2)}) collective-permute-start(bf16[30,16,128]{2,1,0:T(8,128)(2,1)S(1)} %get-tuple-element.36.refs_0_), channel_id=1, source_target_pairs={{0,4},{1,5},{2,6},{3,7},{4,0},{5,1},{6,2},{7,3},{8,12},{9,13},{10,... | collective-permute-start | bytes 368648 | tf_op jit(solution)/shard_map/ppermute | solution.py:325
  27.9 4.5 %collective-permute-done.9.refs_1_ = bf16[30,16,128]{2,1,0:T(8,128)(2,1)S(1)} collective-permute-done((bf16[30,16,128]{2,1,0:T(8,128)(2,1)S(1)}, bf16[30,16,128]{2,1,0:T(8,128)(2,1)S(1)}, u32[]{:S(2)}, u32[]{:S(2)}) %collective-permute-start.9) | collective-permute-done | bytes 122912 | tf_op jit(solution)/shard_map/ppermute | solution.py:325
  32.4 0.8 %collective-permute-start.10 = (bf16[25,16,128]{2,1,0:T(8,128)(2,1)S(1)}, bf16[25,16,128]{2,1,0:T(8,128)(2,1)S(1)}, u32[]{:S(2)}, u32[]{:S(2)}) collective-permute-start(bf16[25,16,128]{2,1,0:T(8,128)(2,1)S(1)} %get-tuple-element.38.refs_0_), channel_id=1, source_target_pairs={{0,2},{1,3},{2,0},{3,1},{4,6},{5,7},{6,4},{7,5},{8,10},{9,11},{10,... | collective-permute-start | bytes 307208 | tf_op jit(solution)/shard_map/ppermute | solution.py:325
  33.2 3.9 %collective-permute-done.10.refs_1_ = bf16[25,16,128]{2,1,0:T(8,128)(2,1)S(1)} collective-permute-done((bf16[25,16,128]{2,1,0:T(8,128)(2,1)S(1)}, bf16[25,16,128]{2,1,0:T(8,128)(2,1)S(1)}, u32[]{:S(2)}, u32[]{:S(2)}) %collective-permute-start.10) | collective-permute-done | bytes 102432 | tf_op jit(solution)/shard_map/ppermute | solution.py:325
  37.2 0.0 copy-done
  37.2 0.0 copy-done.1
  37.2 1.8 %shard_map.75.refs_0_ = bf16[45,16,128]{2,1,0:T(8,128)(2,1)S(1)} custom-call(bf16[25,16,128]{2,1,0:T(8,128)(2,1)S(1)} %get-tuple-element.38.refs_0_, bf16[25,16,128]{2,1,0:T(8,128)(2,1)S(1)} %collective-permute-done.10.refs_1_, f32[5,16,128]{2,1,0:T(8,128)S(1)} %get-tuple-element.39.refs_2_, f32[200,800]{1,0:T(8,128)S(1)} %bitcast.4, f32[200,800]{1,0:T(8,128)S(1)} %bitcast.5), custom_call_target="tpu_custom_call" | custom-call | tf_op jit(solution)/shard_map/pallas_call | solution.py:307
  39.0 1.6 %collective-permute-start.11 = (bf16[45,16,128]{2,1,0:T(8,128)(2,1)S(1)}, bf16[45,16,128]{2,1,0:T(8,128)(2,1)S(1)}, u32[]{:S(2)}, u32[]{:S(2)}) collective-permute-start(bf16[45,16,128]{2,1,0:T(8,128)(2,1)S(1)} %shard_map.75.refs_0_), channel_id=1, source_target_pairs={{0,1},{1,0},{2,3},{3,2},{4,5},{5,4},{6,7},{7,6},{8,9},{9,8},{10,11... | collective-permute-start | bytes 552968 | tf_op jit(solution)/shard_map/ppermute | solution.py:325
  40.6 1.5 %collective-permute-start.12 = (bf16[45,16,128]{2,1,0:T(8,128)(2,1)S(1)}, bf16[45,16,128]{2,1,0:T(8,128)(2,1)S(1)}, u32[]{:S(2)}, u32[]{:S(2)}) collective-permute-start(bf16[45,16,128]{2,1,0:T(8,128)(2,1)S(1)} %shard_map.75.refs_0_), channel_id=1, source_target_pairs={{0,16},{1,17},{2,18},{3,19},{4,20},{5,21},{6,22},{7,23},{8,24},{9,... | collective-permute-start | bytes 552968 | tf_op jit(solution)/shard_map/ppermute | solution.py:325
  42.1 0.4 collective-permute-start.13
  42.5 0.0 collective-permute-start.14
  42.5 3.0 %collective-permute-done.11.refs_1_ = bf16[45,16,128]{2,1,0:T(8,128)(2,1)S(1)} collective-permute-done((bf16[45,16,128]{2,1,0:T(8,128)(2,1)S(1)}, bf16[45,16,128]{2,1,0:T(8,128)(2,1)S(1)}, u32[]{:S(2)}, u32[]{:S(2)}) %collective-permute-start.11) | collective-permute-done | bytes 184352 | tf_op jit(solution)/shard_map/ppermute | solution.py:325
  45.5 0.0 collective-permute-start.15
  45.5 0.6 %collective-permute-done.12.refs_2_ = bf16[45,16,128]{2,1,0:T(8,128)(2,1)S(1)} collective-permute-done((bf16[45,16,128]{2,1,0:T(8,128)(2,1)S(1)}, bf16[45,16,128]{2,1,0:T(8,128)(2,1)S(1)}, u32[]{:S(2)}, u32[]{:S(2)}) %collective-permute-start.12) | collective-permute-done | bytes 184352 | tf_op jit(solution)/shard_map/ppermute | solution.py:325
  46.1 0.0 collective-permute-start.16
  46.1 2.4 %collective-permute-done.13.refs_3_ = bf16[45,16,128]{2,1,0:T(8,128)(2,1)S(1)} collective-permute-done((bf16[45,16,128]{2,1,0:T(8,128)(2,1)S(1)}, bf16[45,16,128]{2,1,0:T(8,128)(2,1)S(1)}, u32[]{:S(2)}, u32[]{:S(2)}) %collective-permute-start.13) | collective-permute-done | bytes 184352 | tf_op jit(solution)/shard_map/ppermute | solution.py:325
  48.5 0.0 collective-permute-start.17
  48.5 0.0 collective-permute-done.14.refs_4_
  48.5 0.0 collective-permute-done.15.refs_5_
  48.6 0.0 collective-permute-done.16.refs_6_
  48.6 1.4 %collective-permute-done.17.refs_7_ = bf16[45,16,128]{2,1,0:T(8,128)(2,1)S(1)} collective-permute-done((bf16[45,16,128]{2,1,0:T(8,128)(2,1)S(1)}, bf16[45,16,128]{2,1,0:T(8,128)(2,1)S(1)}, u32[]{:S(2)}, u32[]{:S(2)}) %collective-permute-start.17) | collective-permute-done | bytes 184352 | tf_op jit(solution)/shard_map/ppermute | solution.py:325
  50.0 3.9 %shard_map.76 = (f32[200,100]{1,0:T(8,128)}, f32[200,100]{1,0:T(8,128)}, bf16[800,800]{1,0:T(8,128)(2,1)}) custom-call(bf16[45,16,128]{2,1,0:T(8,128)(2,1)S(1)} %shard_map.75.refs_0_, bf16[45,16,128]{2,1,0:T(8,128)(2,1)S(1)} %collective-permute-done.11.refs_1_, bf16[45,16,128]{2,1,0:T(8,128)(2,1)S(1)} %collective-permute-done.12.refs_2_, ...), custom_call_target="tpu_custom_call" | custom-call | tf_op jit(solution)/shard_map/pallas_call | solution.py:307
  (1 shorter events, 0.0 us)
Async XLA Ops:
  5.0 2.3 %collective-permute-start = (bf16[4,2,20,16,128]{4,3,2,1,0:T(8,128)(2,1)S(1)}, bf16[4,2,20,16,128]{4,3,2,1,0:T(8,128)(2,1)S(1)}, u32[]{:S(2)}, u32[]{:S(2)}) collective-permute-start(bf16[4,2,20,16,128]{4,3,2,1,0:T(8,128)(2,1)S(1)} %get-tuple-element.24.refs_1_), channel_id=1, source_target_pairs={{0,8},{1,9},{2,10},{3,11},{4,12},{5,13},{6,14},{7,15},{8,0},{9,1},... | collective-permute-start | bytes 1966088 | tf_op jit(solution)/shard_map/ppermute | solution.py:325
  6.9 6.4 %collective-permute-start.4 = (bf16[4,20,16,128]{3,2,1,0:T(8,128)(2,1)S(1)}, bf16[4,20,16,128]{3,2,1,0:T(8,128)(2,1)S(1)}, u32[]{:S(2)}, u32[]{:S(2)}) collective-permute-start(bf16[4,20,16,128]{3,2,1,0:T(8,128)(2,1)S(1)} %shard_map.68.after_ref), channel_id=1, source_target_pairs={{0,8},{1,9},{2,10},{3,11},{4,12},{5,13},{6,14},{7,15},{8,0},{9,1},... | collective-permute-start | bytes 983048 | tf_op jit(solution)/shard_map/ppermute | solution.py:325
  7.4 9.4 %collective-permute-start.1 = (bf16[2,20,16,128]{3,2,1,0:T(8,128)(2,1)S(1)}, bf16[2,20,16,128]{3,2,1,0:T(8,128)(2,1)S(1)}, u32[]{:S(2)}, u32[]{:S(2)}) collective-permute-start(bf16[2,20,16,128]{3,2,1,0:T(8,128)(2,1)S(1)} %get-tuple-element.27), channel_id=1, source_target_pairs={{0,17},{1,16},{2,19},{3,18},{4,21},{5,20},{6,23},{7,22},{8,25},{9,... | collective-permute-start | bytes 491528 | tf_op jit(solution)/shard_map/ppermute | solution.py:325
  11.3 9.1 %collective-permute-start.2 = (bf16[2,20,16,128]{3,2,1,0:T(8,128)(2,1)S(1)}, bf16[2,20,16,128]{3,2,1,0:T(8,128)(2,1)S(1)}, u32[]{:S(2)}, u32[]{:S(2)}) collective-permute-start(bf16[2,20,16,128]{3,2,1,0:T(8,128)(2,1)S(1)} %get-tuple-element.28), channel_id=1, source_target_pairs={{0,16},{1,17},{2,18},{3,19},{4,20},{5,21},{6,22},{7,23},{8,24},{9,... | collective-permute-start | bytes 491528 | tf_op jit(solution)/shard_map/ppermute | solution.py:325
  11.8 8.6 %collective-permute-start.3 = (bf16[2,20,16,128]{3,2,1,0:T(8,128)(2,1)S(1)}, bf16[2,20,16,128]{3,2,1,0:T(8,128)(2,1)S(1)}, u32[]{:S(2)}, u32[]{:S(2)}) collective-permute-start(bf16[2,20,16,128]{3,2,1,0:T(8,128)(2,1)S(1)} %get-tuple-element.29), channel_id=1, source_target_pairs={{0,1},{1,0},{2,3},{3,2},{4,5},{5,4},{6,7},{7,6},{8,9},{9,8},{10,11... | collective-permute-start | bytes 491528 | tf_op jit(solution)/shard_map/ppermute | solution.py:325
  13.3 23.9 %copy-start = (f32[800,200]{0,1:T(8,128)S(1)}, f32[800,200]{0,1:T(8,128)}, u32[]{:S(2)}) copy-start(f32[800,200]{0,1:T(8,128)} %param.6) | copy-start | bytes 1920004
  13.3 23.9 %copy-start.1 = (f32[800,200]{0,1:T(8,128)S(1)}, f32[800,200]{0,1:T(8,128)}, u32[]{:S(2)}) copy-start(f32[800,200]{0,1:T(8,128)} %param.7) | copy-start | bytes 1920004
  13.4 9.0 %collective-permute-start.6 = (bf16[20,16,128]{2,1,0:T(8,128)(2,1)S(1)}, bf16[20,16,128]{2,1,0:T(8,128)(2,1)S(1)}, u32[]{:S(2)}, u32[]{:S(2)}) collective-permute-start(bf16[20,16,128]{2,1,0:T(8,128)(2,1)S(1)} %get-tuple-element.33), channel_id=1, source_target_pairs={{0,17},{1,16},{2,19},{3,18},{4,21},{5,20},{6,23},{7,22},{8,25},{9,... | collective-permute-start | bytes 245768 | tf_op jit(solution)/shard_map/ppermute | solution.py:325
  16.3 6.8 %collective-permute-start.7 = (bf16[20,16,128]{2,1,0:T(8,128)(2,1)S(1)}, bf16[20,16,128]{2,1,0:T(8,128)(2,1)S(1)}, u32[]{:S(2)}, u32[]{:S(2)}) collective-permute-start(bf16[20,16,128]{2,1,0:T(8,128)(2,1)S(1)} %get-tuple-element.34), channel_id=1, source_target_pairs={{0,16},{1,17},{2,18},{3,19},{4,20},{5,21},{6,22},{7,23},{8,24},{9,... | collective-permute-start | bytes 245768 | tf_op jit(solution)/shard_map/ppermute | solution.py:325
  16.8 6.3 %collective-permute-start.8 = (bf16[20,16,128]{2,1,0:T(8,128)(2,1)S(1)}, bf16[20,16,128]{2,1,0:T(8,128)(2,1)S(1)}, u32[]{:S(2)}, u32[]{:S(2)}) collective-permute-start(bf16[20,16,128]{2,1,0:T(8,128)(2,1)S(1)} %get-tuple-element.35), channel_id=1, source_target_pairs={{0,1},{1,0},{2,3},{3,2},{4,5},{5,4},{6,7},{7,6},{8,9},{9,8},{10,11... | collective-permute-start | bytes 245768 | tf_op jit(solution)/shard_map/ppermute | solution.py:325
  20.5 4.5 %collective-permute-start.5 = (bf16[20,16,128]{2,1,0:T(8,128)(2,1)S(1)}, bf16[20,16,128]{2,1,0:T(8,128)(2,1)S(1)}, u32[]{:S(2)}, u32[]{:S(2)}) collective-permute-start(bf16[20,16,128]{2,1,0:T(8,128)(2,1)S(1)} %get-tuple-element.32), channel_id=1, source_target_pairs={{0,2},{1,3},{2,0},{3,1},{4,6},{5,7},{6,4},{7,5},{8,10},{9,11},{10,... | collective-permute-start | bytes 245768 | tf_op jit(solution)/shard_map/ppermute | solution.py:325
  25.0 7.4 %collective-permute-start.9 = (bf16[30,16,128]{2,1,0:T(8,128)(2,1)S(1)}, bf16[30,16,128]{2,1,0:T(8,128)(2,1)S(1)}, u32[]{:S(2)}, u32[]{:S(2)}) collective-permute-start(bf16[30,16,128]{2,1,0:T(8,128)(2,1)S(1)} %get-tuple-element.36.refs_0_), channel_id=1, source_target_pairs={{0,4},{1,5},{2,6},{3,7},{4,0},{5,1},{6,2},{7,3},{8,12},{9,13},{10,... | collective-permute-start | bytes 368648 | tf_op jit(solution)/shard_map/ppermute | solution.py:325
  32.4 4.7 %collective-permute-start.10 = (bf16[25,16,128]{2,1,0:T(8,128)(2,1)S(1)}, bf16[25,16,128]{2,1,0:T(8,128)(2,1)S(1)}, u32[]{:S(2)}, u32[]{:S(2)}) collective-permute-start(bf16[25,16,128]{2,1,0:T(8,128)(2,1)S(1)} %get-tuple-element.38.refs_0_), channel_id=1, source_target_pairs={{0,2},{1,3},{2,0},{3,1},{4,6},{5,7},{6,4},{7,5},{8,10},{9,11},{10,... | collective-permute-start | bytes 307208 | tf_op jit(solution)/shard_map/ppermute | solution.py:325
  39.0 6.5 %collective-permute-start.11 = (bf16[45,16,128]{2,1,0:T(8,128)(2,1)S(1)}, bf16[45,16,128]{2,1,0:T(8,128)(2,1)S(1)}, u32[]{:S(2)}, u32[]{:S(2)}) collective-permute-start(bf16[45,16,128]{2,1,0:T(8,128)(2,1)S(1)} %shard_map.75.refs_0_), channel_id=1, source_target_pairs={{0,1},{1,0},{2,3},{3,2},{4,5},{5,4},{6,7},{7,6},{8,9},{9,8},{10,11... | collective-permute-start | bytes 552968 | tf_op jit(solution)/shard_map/ppermute | solution.py:325
  40.6 5.5 %collective-permute-start.12 = (bf16[45,16,128]{2,1,0:T(8,128)(2,1)S(1)}, bf16[45,16,128]{2,1,0:T(8,128)(2,1)S(1)}, u32[]{:S(2)}, u32[]{:S(2)}) collective-permute-start(bf16[45,16,128]{2,1,0:T(8,128)(2,1)S(1)} %shard_map.75.refs_0_), channel_id=1, source_target_pairs={{0,16},{1,17},{2,18},{3,19},{4,20},{5,21},{6,22},{7,23},{8,24},{9,... | collective-permute-start | bytes 552968 | tf_op jit(solution)/shard_map/ppermute | solution.py:325
  42.1 6.4 %collective-permute-start.13 = (bf16[45,16,128]{2,1,0:T(8,128)(2,1)S(1)}, bf16[45,16,128]{2,1,0:T(8,128)(2,1)S(1)}, u32[]{:S(2)}, u32[]{:S(2)}) collective-permute-start(bf16[45,16,128]{2,1,0:T(8,128)(2,1)S(1)} %shard_map.75.refs_0_), channel_id=1, source_target_pairs={{0,17},{1,16},{2,19},{3,18},{4,21},{5,20},{6,23},{7,22},{8,25},{9,... | collective-permute-start | bytes 552968 | tf_op jit(solution)/shard_map/ppermute | solution.py:325
  42.5 6.0 %collective-permute-start.14 = (bf16[45,16,128]{2,1,0:T(8,128)(2,1)S(1)}, bf16[45,16,128]{2,1,0:T(8,128)(2,1)S(1)}, u32[]{:S(2)}, u32[]{:S(2)}) collective-permute-start(bf16[45,16,128]{2,1,0:T(8,128)(2,1)S(1)} %shard_map.75.refs_0_), channel_id=1, source_target_pairs={{0,8},{1,9},{2,10},{3,11},{4,12},{5,13},{6,14},{7,15},{8,0},{9,1},... | collective-permute-start | bytes 552968 | tf_op jit(solution)/shard_map/ppermute | solution.py:325
  45.5 3.0 %collective-permute-start.15 = (bf16[45,16,128]{2,1,0:T(8,128)(2,1)S(1)}, bf16[45,16,128]{2,1,0:T(8,128)(2,1)S(1)}, u32[]{:S(2)}, u32[]{:S(2)}) collective-permute-start(bf16[45,16,128]{2,1,0:T(8,128)(2,1)S(1)} %collective-permute-done.11.refs_1_), channel_id=1, source_target_pairs={{0,8},{1,9},{2,10},{3,11},{4,12},{5,13},{6,14},{7,15},{8,0},{9,1},... | collective-permute-start | bytes 552968 | tf_op jit(solution)/shard_map/ppermute | solution.py:325
  46.1 2.4 %collective-permute-start.16 = (bf16[45,16,128]{2,1,0:T(8,128)(2,1)S(1)}, bf16[45,16,128]{2,1,0:T(8,128)(2,1)S(1)}, u32[]{:S(2)}, u32[]{:S(2)}) collective-permute-start(bf16[45,16,128]{2,1,0:T(8,128)(2,1)S(1)} %collective-permute-done.12.refs_2_), channel_id=1, source_target_pairs={{0,8},{1,9},{2,10},{3,11},{4,12},{5,13},{6,14},{7,15},{8,0},{9,1},... | collective-permute-start | bytes 552968 | tf_op jit(solution)/shard_map/ppermute | solution.py:325
  48.5 1.4 %collective-permute-start.17 = (bf16[45,16,128]{2,1,0:T(8,128)(2,1)S(1)}, bf16[45,16,128]{2,1,0:T(8,128)(2,1)S(1)}, u32[]{:S(2)}, u32[]{:S(2)}) collective-permute-start(bf16[45,16,128]{2,1,0:T(8,128)(2,1)S(1)} %collective-permute-done.13.refs_3_), channel_id=1, source_target_pairs={{0,8},{1,9},{2,10},{3,11},{4,12},{5,13},{6,14},{7,15},{8,0},{9,1},... | collective-permute-start | bytes 552968 | tf_op jit(solution)/shard_map/ppermute | solution.py:325

commit v2 on v1

--- a/solution.py
+++ b/solution.py
@@ -57,12 +57,10 @@
     def lane(self):
         return lax.broadcasted_iota(jnp.int32, (self.block, LANES), 1)
 
-    def pack_pair(self, tiles, h):
-        if h == 0:
-            sent, rest, start = list(tiles[:-1]), tiles[-1], 0
-        else:
-            mixed = jnp.where(self.lane() < self.tail, tiles[-1], tiles[0])
-            sent, rest, start = [mixed] + list(tiles[1:-1]), tiles[-1], self.tail
+    def pack_pair(self, tiles, high):
+        free = jnp.where(high, self.tail, 0)
+        mixed = jnp.where(self.lane() < free, tiles[-1], tiles[0])
+        rest = jnp.where(high, turn(tiles[-1], -self.tail), tiles[-1])
         groups = -(-self.block // self.fold_rows)
         short = groups * self.fold_rows - self.block
         if short:
@@ -70,10 +68,9 @@
         lane = lax.broadcasted_iota(jnp.int32, (self.fold_rows, LANES), 1)
         folded = jnp.zeros((self.fold_rows, LANES), F32)
         for i in range(groups):
-            piece = rest[i * self.fold_rows:(i + 1) * self.fold_rows]
-            piece = turn(piece, i * self.tail - start)
+            piece = turn(rest[i * self.fold_rows:(i + 1) * self.fold_rows], i * self.tail)
             folded = jnp.where(lane // self.tail == i, piece, folded)
-        stacked = jnp.concatenate(sent + [folded], 0)
+        stacked = jnp.concatenate([mixed] + list(tiles[1:-1]) + [folded], 0)
         left = self.grad_rows - stacked.shape[0]
         if left:
             stacked = jnp.concatenate([stacked, jnp.zeros((left, LANES), F32)], 0)
@@ -93,16 +90,6 @@
         last = jnp.where(self.lane() < self.tail, sent[0], rest)
         return sent + [last]
 
-    def tiles_of(self, rows, h):
-        start = h * self.tiles * LANES
-        stop = min(start + (self.tiles + 1) * LANES, self.width)
-        tiles = [rows[:, at:min(at + LANES, stop)] for at in range(start, stop, LANES)]
-        missing = LANES - tiles[-1].shape[1]
-        if missing:
-            pad = jnp.zeros((self.block, missing), F32)
-            tiles[-1] = jnp.concatenate([tiles[-1], pad], 1)
-        return tiles
-
     def pack_cov(self, matrix):
         corner = matrix[LANES:, LANES:]
         corner = jnp.concatenate([corner, jnp.zeros((self.corner, LANES - self.corner), F32)], 1)
@@ -122,8 +109,33 @@
     return seq, core, xy, owner_block
 
 
-def grad_kernel(plan, x_ref, y_ref, keep_ref, send_ref, both_ref, sems):
+def grad_half(plan, other, turned, both_ref, keep_ref, send_ref):
     _, core, xy, _ = place(plan)
+    high = (xy + other) % 2 == 1
+    span = (plan.tiles + 1) * LANES
+    start = plan.tiles * LANES
+    late = both_ref[1, :, start:]
+    missing = span - late.shape[1]
+    if missing:
+        late = jnp.concatenate([late, jnp.zeros((plan.tokens, missing), BF16)], 1)
+    part = jnp.where(high, late, both_ref[1, :, :span])
+    grad = dot(turned, part, NN)
+    for b in range(plan.blocks):
+        rows = grad[b * plan.block:(b + 1) * plan.block]
+        tiles = [rows[:, k * LANES:(k + 1) * LANES] for k in range(plan.tiles + 1)]
+        packed = plan.pack_pair(tiles, high)
+        j = b % 2 ^ xy // 2
+
+        @pl.when(core == b // 2)
+        def _():
+            keep_ref[j] = packed
+
+        @pl.when(core != b // 2)
+        def _():
+            send_ref[j] = packed.astype(BF16)
+
+
+def far_kernel(plan, x_ref, y_ref, keep_ref, send_ref, both_ref, turned_ref, sems):
     copies = [
         pltpu.make_async_copy(x_ref, both_ref.at[0], sems.at[0]),
         pltpu.make_async_copy(y_ref, both_ref.at[1], sems.at[1]),
@@ -132,21 +144,13 @@
         copy.start()
     copies[0].wait()
     turned = both_ref[0].T
+    turned_ref[...] = turned
     copies[1].wait()
-    grad = dot(turned, both_ref[1], NN)
-    for b in range(plan.blocks):
-        rows = grad[b * plan.block:(b + 1) * plan.block]
-        for h in range(2):
-            packed = plan.pack_pair(plan.tiles_of(rows, h), h)
-            j = (b % 2 * 2 + h) ^ xy
-
-            @pl.when(core == b // 2)
-            def _():
-                keep_ref[j] = packed
-
-            @pl.when(core != b // 2)
-            def _():
-                send_ref[j] = packed.astype(BF16)
+    grad_half(plan, 1, turned, both_ref, keep_ref, send_ref)
+
+
+def near_kernel(plan, both_ref, turned_ref, keep_ref, send_ref):
+    grad_half(plan, 0, turned_ref[...], both_ref, keep_ref, send_ref)
 
 
 def cov_kernel(plan, mine, both_ref, after_ref, out_ref):
@@ -162,6 +166,16 @@
             out_ref[t ^ xy, pl.ds(slot, piece.shape[0])] = piece.astype(out_ref.dtype)
 
 
+def far_split_kernel(keep_ref, recv_ref, after_ref, y_ref, d_ref):
+    for j, ref in enumerate((y_ref, d_ref)):
+        ref[...] = (keep_ref[j] + recv_ref[j].astype(F32)).astype(BF16)
+
+
+def near_split_kernel(keep_ref, recv_ref, after_ref, own_ref, x_ref):
+    own_ref[...] = keep_ref[0] + recv_ref[0].astype(F32)
+    x_ref[...] = (keep_ref[1] + recv_ref[1].astype(F32)).astype(BF16)
+
+
 def split_kernel(keep_ref, recv_ref, after_ref, own_ref, *send_refs):
     own_ref[...] = keep_ref[0] + recv_ref[0].astype(F32)
     for j in range(1, 4):
@@ -208,12 +222,6 @@
     return high, (value - high.astype(F32)).astype(BF16)
 
 
-def dot_split(a, b, dims):
-    a_high, a_low = split_two(a)
-    b_high, b_low = split_two(b)
-    return dot(a_high, b_high, dims) + (dot(a_high, b_low, dims) + dot(a_low, b_high, dims))
-
-
 def pick(ref, plan, wanted):
     value = ref[:, :plan.block]
     for n in range(1, plan.blocks):
@@ -221,83 +229,100 @@
     return value
 
 
+def inverses_kernel(plan, p_ref, q_ref, after_ref, p_out, q_out):
+    _, core, xy, _ = place(plan)
+    high, low = split_two(pick(p_ref, plan, core * 2 + xy // 2).T)
+    p_out[0], p_out[1] = high, low
+    for e in range(2):
+        high, low = split_two(pick(q_ref, plan, xy % 2 * 2 + e))
+        q_out[e, 0], q_out[e, 1] = high, low
+
+
 def finish_kernel(plan, mine_ref, recv_ref, cov_ref, p_ref, q_ref, out_ref, whole):
-    _, core, xy, owner_block = place(plan)
+    _, _, xy, owner_block = place(plan)
     g, c, block = plan.g, plan.c, plan.block
     cov = cov_ref[...] + recv_ref[pl.ds(g, c)].astype(F32)
     out_ref[pl.ds(2 * g, c)] = cov.astype(BF16)
     whole[owner_block % 2] = mine_ref[pl.ds(0, g)].astype(F32)
     whole[1 - owner_block % 2] = recv_ref[pl.ds(0, g)].astype(F32)
-    low = xy % 2 == 0
+    high = xy % 2 == 1
     pair = whole[...]
-    natural = [jnp.concatenate(plan.unpack_pair(pair, h), 1).astype(BF16) for h in range(2)]
-    p_high, p_low = split_two(pick(p_ref, plan, core * 2 + xy // 2).T)
+    natural = [jnp.concatenate(plan.unpack_pair(pair, h), 1) for h in range(2)]
+    part = jnp.where(high, natural[1][:, plan.tail:plan.tail + 2 * block],
+                     natural[0][:, :2 * block]).astype(BF16)
+    left = dot(p_ref[0], part, NN) + dot(p_ref[1], part, NN)
     done = []
     for e in range(2):
-        at = e * block
-        part = jnp.where(low, natural[0][:, at:at + block].astype(F32),
-                         natural[1][:, at + plan.tail:at + plan.tail + block].astype(F32))
-        part = part.astype(BF16)
-        left = dot(p_high, part, NN) + dot(p_low, part, NN)
-        done.append(dot_split(left, pick(q_ref, plan, xy % 2 * 2 + e), NT) * (1.0 / plan.count))
+        l_high, l_low = split_two(left[:, e * block:(e + 1) * block])
+        value = dot(l_high, q_ref[e, 0], NT) + (
+            dot(l_high, q_ref[e, 1], NT) + dot(l_low, q_ref[e, 0], NT))
+        done.append(value * (1.0 / plan.count))
     tail = jnp.zeros((block, plan.tail), F32)
     end = jnp.zeros((block, LANES - 2 * plan.tail), F32)
-    packed = []
-    for h, order in ((0, done + [tail, end]), (1, [tail] + done + [end])):
-        row = jnp.concatenate(order, 1)
-        tiles = [row[:, k * LANES:(k + 1) * LANES] for k in range(plan.tiles + 1)]
-        packed.append(plan.pack_pair(tiles, h))
-    packed = jnp.where(low, packed[0], packed[1]).astype(BF16)
+    row = jnp.where(high, jnp.concatenate([tail] + done + [end], 1),
+                    jnp.concatenate(done + [tail, end], 1))
+    tiles = [row[:, k * LANES:(k + 1) * LANES] for k in range(plan.tiles + 1)]
+    packed = plan.pack_pair(tiles, high).astype(BF16)
     out_ref[pl.ds(0, 2 * g)] = packed.reshape(2 * g, PACK, LANES)
 
 
-def assemble_kernel(plan, *refs):
-    bundles, (in_ref, out_ref, grad_ref, whole, done, sems, out_sems) = refs[:8], refs[8:]
+def assemble(plan, away, bundles, grad_ref, covs, done, sems):
     seq, core, xy, _ = place(plan)
-    g, block = plan.g, plan.block
-    copies = []
-    for i in range(8):
-        q = (core ^ (i // 4)) * 4 + (xy ^ (i % 4))
-        copies.append(pltpu.make_async_copy(bundles[i], whole.at[q], sems.at[i]))
-    for copy in copies:
-        copy.start()
-    for copy in copies:
-        copy.wait()
+    g, c, block = plan.g, plan.c, plan.block
+    even = xy % 2 == 0
     writes = []
-    for b in range(plan.blocks):
-        low, high = (
-            plan.unpack_pair(whole[2 * b + h, pl.ds(0, 2 * g)].astype(F32), h) for h in range(2))
+    for k in range(2):
+        first, second = (bundles[2 * k + e][pl.ds(0, 2 * g)] for e in range(2))
+        low = plan.unpack_pair(jnp.where(even, first, second).astype(F32), 0)
+        high = plan.unpack_pair(jnp.where(even, second, first).astype(F32), 1)
         middle = jnp.where(plan.lane() < plan.tail, low[-1], high[0])
         row = low[:-1] + [middle] + high[1:-1] + [high[-1][:, :2 * plan.tail]]
-        done[b] = jnp.concatenate(row, 1).astype(BF16)
+        done[k] = jnp.concatenate(row, 1).astype(BF16)
+        b = (core ^ away) * 2 + (xy // 2 ^ k)
         write = pltpu.make_async_copy(
-            done.at[b], grad_ref.at[pl.ds(b * block, block)], out_sems.at[b])
+            done.at[k], grad_ref.at[pl.ds(pl.multiple_of(b * block, 8), block)], sems.at[k])
         write.start()
         writes.append(write)
-    first = (seq % (plan.ns // plan.blocks)) * plan.owned
-    row = lax.broadcasted_iota(jnp.int32, (plan.owned, block), 0) + first
+    for j in range(4):
+        covs[j ^ xy] = bundles[j][pl.ds(2 * g, c)]
+    start = (seq % (plan.ns // plan.blocks)) * plan.owned
+    row = lax.broadcasted_iota(jnp.int32, (plan.owned, block), 0) + start
     column = lax.broadcasted_iota(jnp.int32, (plan.owned, block), 1)
     select = jnp.where(row == column, 1.0, 0.0).astype(BF16)
     r128 = lax.broadcasted_iota(jnp.int32, (LANES, LANES), 0)
     c128 = lax.broadcasted_iota(jnp.int32, (LANES, LANES), 1)
     eye = jnp.where(r128 == c128, 1.0, 0.0).astype(BF16)
-    for factor, ref in ((0, in_ref), (1, out_ref)):
-        pieces = [
-            whole[factor * 4 + t, pl.ds(2 * g, plan.cuts[t + 1] - plan.cuts[t])].astype(F32)
-            for t in range(4)
-        ]
-        stacked = jnp.concatenate(pieces, 0).reshape(plan.cov_total, LANES)
-        left = stacked[:block]
-        corner = stacked[block:block + plan.corner, :plan.corner]
-        top = dot(eye, left[LANES:].astype(BF16), NT)
-        right = jnp.concatenate([top, corner], 0)
-        both = jnp.concatenate([left, right], 1).astype(BF16)
-        ref[...] = dot(both, select, NT) * (1.0 / plan.count)
+    pieces = [covs[t, pl.ds(0, plan.cuts[t + 1] - plan.cuts[t])].astype(F32) for t in range(4)]
+    stacked = jnp.concatenate(pieces, 0).reshape(plan.cov_total, LANES)
+    left = stacked[:block]
+    corner = stacked[block:block + plan.corner, :plan.corner]
+    top = dot(eye, left[LANES:].astype(BF16), NT)
+    right = jnp.concatenate([top, corner], 0)
+    whole = jnp.concatenate([left, right], 1).astype(BF16)
+    factor = dot(whole, select, NT) * (1.0 / plan.count)
+    return factor, writes
+
+
+def home_kernel(plan, *refs):
+    bundles, (grad_ref, factor_ref, covs, done, sems) = refs[:4], refs[4:]
+    factor_ref[...], writes = assemble(plan, 0, bundles, grad_ref, covs, done, sems)
     for write in writes:
         write.wait()
 
 
-def call(kernel, shapes, args, scratch=(), hbm_in=0, hbm_out=()):
+def away_kernel(plan, *refs):
+    _, mine_ref, *bundles = refs[:6]
+    grad_ref, in_ref, out_ref, covs, done, sems = refs[6:]
+    core = place(plan)[1]
+    mine = mine_ref[...]
+    theirs, writes = assemble(plan, 1, bundles, grad_ref, covs, done, sems)
+    in_ref[...] = jnp.where(core == 0, mine, theirs)
+    out_ref[...] = jnp.where(core == 0, theirs, mine)
+    for write in writes:
+        write.wait()
+
+
+def call(kernel, shapes, args, scratch=(), hbm_in=0, hbm_out=0, aliases=None):
     vmem = pl.BlockSpec(memory_space=pltpu.VMEM)
     hbm = pl.BlockSpec(memory_space=pltpu.HBM)
     args = [
@@ -308,9 +333,10 @@
         kernel,
         out_shape=[jax.ShapeDtypeStruct(s, d) for s, d in shapes],
         in_specs=[hbm if i < hbm_in else vmem for i in range(len(args))],
-        out_specs=[hbm if i in hbm_out else vmem for i in range(len(shapes))],
+        out_specs=[hbm if i < hbm_out else vmem for i in range(len(shapes))],
         scratch_shapes=list(scratch),
         compiler_params=pltpu.CompilerParams(vmem_limit_bytes=VMEM_LIMIT),
+        input_output_aliases=aliases or {},
     )(*args)
 
 
@@ -347,13 +373,6 @@
         def units(n, dtype, *lead):
             return (*lead, n, PACK, LANES), dtype
 
-        def exchange_parts(keep, send, after, shape):
-            own, *sends = call(
-                split_kernel, [(shape, F32)] + [(shape, BF16)] * 3,
-                (keep, swap(send, 1, 0), after))
-            peers = [swap(sends[2], 2, 1), swap(sends[1], 2, 0), swap(sends[0], 0, 1)]
-            return [own] + peers
-
         def widen(parts, shape):
             for batch_bit, seq_bit in extra:
                 summed, = call(sum_kernel, [(shape, BF16)], parts)
@@ -361,19 +380,38 @@
             return parts
 
         tile = (PACK, LANES)
-        keep, send, both = call(
-            bind(grad_kernel),
-            [units(g, F32, 4, 2), units(g, BF16, 4, 2), ((2, tokens, width), BF16)],
+        far_keep, far_send, both, turned = call(
+            bind(far_kernel),
+            [units(g, F32, 2, 2), units(g, BF16, 2, 2), ((2, tokens, width), BF16),
+             ((width, tokens), BF16)],
             (layer_inputs, output_grads), hbm_in=2,
             scratch=[pltpu.SemaphoreType.DMA((2,))])
+        far_recv = swap(far_send, 1, 0)
+        near_keep, near_send = call(
+            bind(near_kernel), [units(g, F32, 2, 2), units(g, BF16, 2, 2)],
+            (both, turned))
+        near_recv = swap(near_send, 1, 0)
+        y_send, d_send = call(
+            far_split_kernel, [units(g, BF16, 2)] * 2,
+            (far_keep, far_recv, near_send))
+        y_recv, d_recv = swap(y_send, 0, 1), swap(d_send, 2, 1)
+        own, x_send = call(
+            near_split_kernel, [units(g, F32, 2), units(g, BF16, 2)],
+            (near_keep, near_recv, y_send))
+        x_recv = swap(x_send, 2, 0)
+        parts = [own, y_recv, d_recv, x_recv]
         cov_send, = call(
             group(lambda refs, outs: cov_kernel(plan, False, *refs, *outs), 1),
-            [units(4 * c, BF16, 4)], (both, send))
-        parts = exchange_parts(keep, send, cov_send, (2, g, *tile))
+            [units(4 * c, BF16, 4)], (both, own))
+        cov_recv = swap(cov_send, 1, 0)
         cov_keep, = call(
             group(lambda refs, outs: cov_kernel(plan, True, *refs, *outs), 1),
-            [units(4 * c, F32, 4)], (both, parts[0]))
-        cov_parts = exchange_parts(cov_keep, cov_send, parts[0], (4 * c, *tile))
+            [units(4 * c, F32, 4)], (both, cov_send))
+        cov_own, *cov_sends = call(
+            split_kernel, [units(4 * c, F32)] + [units(4 * c, BF16)] * 3,
+            (cov_keep, cov_recv, own))
+        cov_parts = [cov_own, swap(cov_sends[0], 0, 1), swap(cov_sends[1], 2, 0),
+                     swap(cov_sends[2], 2, 1)]
         send, keep = call(
             group(first_kernel, 2, plan), [units(g, BF16), units(g, F32)],
             widen(parts, (2, g, *tile)) + [cov_parts[0]])
@@ -383,20 +421,25 @@
         send, cov = call(
             bind(third_kernel), [units(g + c, BF16), units(c, F32)],
             (send, swap(send, 0, 2 * step), cov))
+        p_parts, q_parts = call(
+            bind(inverses_kernel),
+            [((2, plan.block, plan.block), BF16), ((2, 2, plan.block, plan.block), BF16)],
+            (input_inverse.T, output_inverse.T, keep))
         done, = call(
             bind(finish_kernel), [units(2 * g + c, BF16)],
-            (send, swap(send, 0, step), cov, input_inverse.T, output_inverse.T),
+            (send, swap(send, 0, step), cov, p_parts, q_parts),
             scratch=[pltpu.VMEM(units(g, F32, 2)[0], F32)])
         mine = [done, swap(done, 0, 1), swap(done, 2, 0), swap(done, 2, 1)]
         theirs = [swap(value, 1, 0) for value in mine]
-        in_factor, out_factor, grad = call(
-            bind(assemble_kernel),
-            [((plan.block, plan.owned), F32)] * 2 + [((width, width), BF16)],
-            mine + theirs, hbm_out=(2,),
-            scratch=[
-                pltpu.VMEM(units(2 * g + c, BF16, 8)[0], BF16),
-                pltpu.VMEM((plan.blocks, plan.block, width), BF16),
-                pltpu.SemaphoreType.DMA((8,)), pltpu.SemaphoreType.DMA((plan.blocks,))])
+        staging = [
+            pltpu.VMEM(units(c, BF16, 4)[0], BF16), pltpu.VMEM((2, plan.block, width), BF16),
+            pltpu.SemaphoreType.DMA((2,))]
+        result, factor = ((width, width), BF16), ((plan.block, plan.owned), F32)
+        grad, home = call(
+            bind(home_kernel), [result, factor], mine, hbm_out=1, scratch=staging)
+        grad, in_factor, out_factor = call(
+            bind(away_kernel), [result, factor, factor], [grad, home] + theirs,
+            hbm_in=1, hbm_out=1, aliases={0: 0}, scratch=staging)
         return in_factor.T, out_factor.T, grad
 
     return jax.shard_map(

time: 54.1 us -> 54.7 us (1.011)
    ppermute x18 -> x19, waiting for transfers between devices: 20.8 us -> 21.3 us  [swap(): return lax.ppermute(value, AXES, pairs)]
    pallas_call x10 -> x14, Pallas kernels: 13.1 us -> 13.2 us  [call(): pl.pallas_call(kernel, out_shape=[jax.ShapeDtypeStruct(s, d) for s, d in...]
    ppermute x18 -> x19, starting transfers between devices: 19.2 us -> 19.3 us  [swap(): return lax.ppermute(value, AXES, pairs)]
  transfers between devices with their start and end apart: 18 -> 19, of which waited for: 10 -> 10; matrix products, arithmetic and copies ran while one was open for 0% -> 0% of each run, Pallas kernels for 5% -> 10%
where the time goes in v2:
time: 54.7 us; the launch traced here: 54.6 us
  waiting for transfers between devices  21.3 us (39%)
  starting transfers between devices  19.3 us (35%)
  Pallas kernels  13.2 us (24%)
  between operations  0.76 us (1%)
    ppermute x19, waiting for transfers between devices, swap(): return lax.ppermute(value, AXES, pairs)  21.3 us
    ppermute x19, starting transfers between devices, swap(): return lax.ppermute(value, AXES, pairs)  19.3 us
    pallas_call x14, Pallas kernels, call(): pl.pallas_call(kernel, out_shape=[jax.ShapeDtypeStruct(s, d) for s, d in...  13.2 us
  transfers between devices with their start and end apart: 19, of which 10 were waited for; matrix products, arithmetic and copies ran while one was open for 0% of the time, Pallas kernels for 10%

profile of v2, /device:TPU:0, one launch (start us, length us, event | category | flops | bytes accessed | tf_op | source)
XLA Modules:
  0.0 54.6 jit_solution(12625731572791988750)
XLA Ops:
  0.6 3.4 %shard_map.67 = (f32[2,2,20,16,128]{4,3,2,1,0:T(8,128)S(1)}, bf16[2,2,20,16,128]{4,3,2,1,0:T(8,128)(2,1)S(1)}, bf16[2,800,800]{2,1,0:T(8,128)(2,1)S(1)}, bf16[800,800]{1,0:T(8,128)(2,1)S(1)}) custom-call(bf16[800,800]{1,0:T(8,128)(2,1)} %refs_0_.1, bf16[800,800]{1,0:T(8,128)(2,1)} %refs_1_.1), custom_call_target="tpu_custom_call" | custom-call | tf_op jit(solution)/shard_map/pallas_call | solution.py:332
  4.0 0.6 %collective-permute-start.1 = (bf16[2,2,20,16,128]{4,3,2,1,0:T(8,128)(2,1)S(1)}, bf16[2,2,20,16,128]{4,3,2,1,0:T(8,128)(2,1)S(1)}, u32[]{:S(2)}, u32[]{:S(2)}) collective-permute-start(bf16[2,2,20,16,128]{4,3,2,1,0:T(8,128)(2,1)S(1)} %get-tuple-element.35), channel_id=1, source_target_pairs={{0,8},{1,9},{2,10},{3,11},{4,12},{5,13},{6,14},{7,15},{8,0},{9,1},... | collective-permute-start | bytes 983048 | tf_op jit(solution)/shard_map/ppermute | solution.py:351
  4.6 1.6 %shard_map.68 = (f32[2,2,20,16,128]{4,3,2,1,0:T(8,128)S(1)}, bf16[2,2,20,16,128]{4,3,2,1,0:T(8,128)(2,1)S(1)}) custom-call(bf16[2,800,800]{2,1,0:T(8,128)(2,1)S(1)} %get-tuple-element.30.refs_0_, bf16[800,800]{1,0:T(8,128)(2,1)S(1)} %get-tuple-element.31.refs_1_), custom_call_target="tpu_custom_call" | custom-call | tf_op jit(solution)/shard_map/pallas_call | solution.py:332
  6.2 0.1 collective-permute-start
  6.2 0.0 collective-permute-done.1.recv_ref
  6.3 0.1 shard_map.69
  6.3 1.5 %collective-permute-done.recv_ref = bf16[2,2,20,16,128]{4,3,2,1,0:T(8,128)(2,1)S(1)} collective-permute-done((bf16[2,2,20,16,128]{4,3,2,1,0:T(8,128)(2,1)S(1)}, bf16[2,2,20,16,128]{4,3,2,1,0:T(8,128)(2,1)S(1)}, u32[]{:S(2)}, u32[]{:S(2)}) %collective-permute-start) | collective-permute-done | bytes 327712 | tf_op jit(solution)/shard_map/ppermute | solution.py:351
  7.9 0.1 shard_map.70
  7.9 1.4 %shard_map.71.refs_1_ = bf16[4,20,16,128]{3,2,1,0:T(8,128)(2,1)S(1)} custom-call(bf16[2,800,800]{2,1,0:T(8,128)(2,1)S(1)} %get-tuple-element.30.refs_0_, f32[2,20,16,128]{3,2,1,0:T(8,128)S(1)} %get-tuple-element.37.refs_1_.after_ref.refs_0_), custom_call_target="tpu_custom_call" | custom-call | tf_op jit(solution)/shard_map/pallas_call | solution.py:332
  9.3 0.2 collective-permute-start.5
  9.5 2.9 %collective-permute-start.4 = (bf16[2,20,16,128]{3,2,1,0:T(8,128)(2,1)S(1)}, bf16[2,20,16,128]{3,2,1,0:T(8,128)(2,1)S(1)}, u32[]{:S(2)}, u32[]{:S(2)}) collective-permute-start(bf16[2,20,16,128]{3,2,1,0:T(8,128)(2,1)S(1)} %get-tuple-element.39), channel_id=1, source_target_pairs={{0,16},{1,17},{2,18},{3,19},{4,20},{5,21},{6,22},{7,23},{8,24},{9,... | collective-permute-start | bytes 491528 | tf_op jit(solution)/shard_map/ppermute | solution.py:351
  12.4 1.5 %collective-permute-start.3 = (bf16[2,20,16,128]{3,2,1,0:T(8,128)(2,1)S(1)}, bf16[2,20,16,128]{3,2,1,0:T(8,128)(2,1)S(1)}, u32[]{:S(2)}, u32[]{:S(2)}) collective-permute-start(bf16[2,20,16,128]{3,2,1,0:T(8,128)(2,1)S(1)} %get-tuple-element.38), channel_id=1, source_target_pairs={{0,17},{1,16},{2,19},{3,18},{4,21},{5,20},{6,23},{7,22},{8,25},{9,... | collective-permute-start | bytes 491528 | tf_op jit(solution)/shard_map/ppermute | solution.py:351
  13.9 0.0 collective-permute-start.2
  13.9 1.4 %shard_map.72.keep_ref = f32[4,20,16,128]{3,2,1,0:T(8,128)S(1)} custom-call(bf16[2,800,800]{2,1,0:T(8,128)(2,1)S(1)} %get-tuple-element.30.refs_0_, bf16[4,20,16,128]{3,2,1,0:T(8,128)(2,1)S(1)} %shard_map.71.refs_1_), custom_call_target="tpu_custom_call" | custom-call | tf_op jit(solution)/shard_map/pallas_call | solution.py:332
  15.3 0.0 copy-start
  15.3 0.0 copy-start.1
  15.3 0.0 collective-permute-done.5.recv_ref
  15.3 0.1 shard_map.73
  15.4 2.1 %collective-permute-start.7 = (bf16[20,16,128]{2,1,0:T(8,128)(2,1)S(1)}, bf16[20,16,128]{2,1,0:T(8,128)(2,1)S(1)}, u32[]{:S(2)}, u32[]{:S(2)}) collective-permute-start(bf16[20,16,128]{2,1,0:T(8,128)(2,1)S(1)} %get-tuple-element.43), channel_id=1, source_target_pairs={{0,1},{1,0},{2,3},{3,2},{4,5},{5,4},{6,7},{7,6},{8,9},{9,8},{10,11... | collective-permute-start | bytes 245768 | tf_op jit(solution)/shard_map/ppermute | solution.py:351
  17.4 1.5 %collective-permute-start.8 = (bf16[20,16,128]{2,1,0:T(8,128)(2,1)S(1)}, bf16[20,16,128]{2,1,0:T(8,128)(2,1)S(1)}, u32[]{:S(2)}, u32[]{:S(2)}) collective-permute-start(bf16[20,16,128]{2,1,0:T(8,128)(2,1)S(1)} %get-tuple-element.44), channel_id=1, source_target_pairs={{0,16},{1,17},{2,18},{3,19},{4,20},{5,21},{6,22},{7,23},{8,24},{9,... | collective-permute-start | bytes 245768 | tf_op jit(solution)/shard_map/ppermute | solution.py:351
  18.9 0.0 collective-permute-done.4.refs_3_
  18.9 1.5 %collective-permute-start.9 = (bf16[20,16,128]{2,1,0:T(8,128)(2,1)S(1)}, bf16[20,16,128]{2,1,0:T(8,128)(2,1)S(1)}, u32[]{:S(2)}, u32[]{:S(2)}) collective-permute-start(bf16[20,16,128]{2,1,0:T(8,128)(2,1)S(1)} %get-tuple-element.45), channel_id=1, source_target_pairs={{0,17},{1,16},{2,19},{3,18},{4,21},{5,20},{6,23},{7,22},{8,25},{9,... | collective-permute-start | bytes 245768 | tf_op jit(solution)/shard_map/ppermute | solution.py:351
  20.4 2.1 %collective-permute-done.3.refs_2_ = bf16[2,20,16,128]{3,2,1,0:T(8,128)(2,1)S(1)} collective-permute-done((bf16[2,20,16,128]{3,2,1,0:T(8,128)(2,1)S(1)}, bf16[2,20,16,128]{3,2,1,0:T(8,128)(2,1)S(1)}, u32[]{:S(2)}, u32[]{:S(2)}) %collective-permute-start.3) | collective-permute-done | bytes 163872 | tf_op jit(solution)/shard_map/ppermute | solution.py:351
  22.5 3.2 %collective-permute-done.2.refs_1_ = bf16[2,20,16,128]{3,2,1,0:T(8,128)(2,1)S(1)} collective-permute-done((bf16[2,20,16,128]{3,2,1,0:T(8,128)(2,1)S(1)}, bf16[2,20,16,128]{3,2,1,0:T(8,128)(2,1)S(1)}, u32[]{:S(2)}, u32[]{:S(2)}) %collective-permute-start.2) | collective-permute-done | bytes 163872 | tf_op jit(solution)/shard_map/ppermute | solution.py:351
  25.7 0.1 shard_map.74
  25.8 1.6 %collective-permute-start.6 = (bf16[20,16,128]{2,1,0:T(8,128)(2,1)S(1)}, bf16[20,16,128]{2,1,0:T(8,128)(2,1)S(1)}, u32[]{:S(2)}, u32[]{:S(2)}) collective-permute-start(bf16[20,16,128]{2,1,0:T(8,128)(2,1)S(1)} %get-tuple-element.42), channel_id=1, source_target_pairs={{0,2},{1,3},{2,0},{3,1},{4,6},{5,7},{6,4},{7,5},{8,10},{9,11},{10,... | collective-permute-start | bytes 245768 | tf_op jit(solution)/shard_map/ppermute | solution.py:351
  27.4 0.0 collective-permute-done.7.refs_3_
  27.4 0.0 collective-permute-done.8.refs_4_
  27.4 0.0 collective-permute-done.9.refs_5_
  27.4 3.6 %collective-permute-done.6.refs_1_ = bf16[20,16,128]{2,1,0:T(8,128)(2,1)S(1)} collective-permute-done((bf16[20,16,128]{2,1,0:T(8,128)(2,1)S(1)}, bf16[20,16,128]{2,1,0:T(8,128)(2,1)S(1)}, u32[]{:S(2)}, u32[]{:S(2)}) %collective-permute-start.6) | collective-permute-done | bytes 81952 | tf_op jit(solution)/shard_map/ppermute | solution.py:351
  31.0 0.1 shard_map.75
  31.1 1.9 %collective-permute-start.10 = (bf16[30,16,128]{2,1,0:T(8,128)(2,1)S(1)}, bf16[30,16,128]{2,1,0:T(8,128)(2,1)S(1)}, u32[]{:S(2)}, u32[]{:S(2)}) collective-permute-start(bf16[30,16,128]{2,1,0:T(8,128)(2,1)S(1)} %get-tuple-element.46.refs_0_), channel_id=1, source_target_pairs={{0,4},{1,5},{2,6},{3,7},{4,0},{5,1},{6,2},{7,3},{8,12},{9,13},{10,... | collective-permute-start | bytes 368648 | tf_op jit(solution)/shard_map/ppermute | solution.py:351
  33.0 4.1 %collective-permute-done.10.refs_1_ = bf16[30,16,128]{2,1,0:T(8,128)(2,1)S(1)} collective-permute-done((bf16[30,16,128]{2,1,0:T(8,128)(2,1)S(1)}, bf16[30,16,128]{2,1,0:T(8,128)(2,1)S(1)}, u32[]{:S(2)}, u32[]{:S(2)}) %collective-permute-start.10) | collective-permute-done | bytes 122912 | tf_op jit(solution)/shard_map/ppermute | solution.py:351
  37.1 1.9 %collective-permute-start.11 = (bf16[25,16,128]{2,1,0:T(8,128)(2,1)S(1)}, bf16[25,16,128]{2,1,0:T(8,128)(2,1)S(1)}, u32[]{:S(2)}, u32[]{:S(2)}) collective-permute-start(bf16[25,16,128]{2,1,0:T(8,128)(2,1)S(1)} %get-tuple-element.48.refs_0_), channel_id=1, source_target_pairs={{0,2},{1,3},{2,0},{3,1},{4,6},{5,7},{6,4},{7,5},{8,10},{9,11},{10,... | collective-permute-start | bytes 307208 | tf_op jit(solution)/shard_map/ppermute | solution.py:351
  39.0 0.0 copy-done
  39.0 0.0 copy-done.1
  39.0 1.1 %shard_map.77 = (bf16[2,200,200]{2,1,0:T(8,128)(2,1)S(1)}, bf16[2,2,200,200]{3,2,1,0:T(8,128)(2,1)S(1)}) custom-call(f32[200,800]{1,0:T(8,128)S(1)} %bitcast.4, f32[200,800]{1,0:T(8,128)S(1)} %bitcast.5, f32[20,16,128]{2,1,0:T(8,128)S(1)} %get-tuple-element.41.refs_0_.refs_2_), custom_call_target="tpu_custom_call" | custom-call | tf_op jit(solution)/shard_map/pallas_call | solution.py:332
  40.1 1.7 %collective-permute-done.11.refs_1_ = bf16[25,16,128]{2,1,0:T(8,128)(2,1)S(1)} collective-permute-done((bf16[25,16,128]{2,1,0:T(8,128)(2,1)S(1)}, bf16[25,16,128]{2,1,0:T(8,128)(2,1)S(1)}, u32[]{:S(2)}, u32[]{:S(2)}) %collective-permute-start.11) | collective-permute-done | bytes 102432 | tf_op jit(solution)/shard_map/ppermute | solution.py:351
  41.8 1.1 %shard_map.78.refs_0_ = bf16[45,16,128]{2,1,0:T(8,128)(2,1)S(1)} custom-call(bf16[25,16,128]{2,1,0:T(8,128)(2,1)S(1)} %get-tuple-element.48.refs_0_, bf16[25,16,128]{2,1,0:T(8,128)(2,1)S(1)} %collective-permute-done.11.refs_1_, f32[5,16,128]{2,1,0:T(8,128)S(1)} %get-tuple-element.49.refs_2_, bf16[2,200,200]{2,1,0:T(8,128)(2,1)S(1)} %get-tuple-element.50.refs_3_, ...), custom_call_target="tpu_custom_call" | custom-call | tf_op jit(solution)/shard_map/pallas_call | solution.py:332
  42.9 1.5 %collective-permute-start.14 = (bf16[45,16,128]{2,1,0:T(8,128)(2,1)S(1)}, bf16[45,16,128]{2,1,0:T(8,128)(2,1)S(1)}, u32[]{:S(2)}, u32[]{:S(2)}) collective-permute-start(bf16[45,16,128]{2,1,0:T(8,128)(2,1)S(1)} %shard_map.78.refs_0_), channel_id=1, source_target_pairs={{0,17},{1,16},{2,19},{3,18},{4,21},{5,20},{6,23},{7,22},{8,25},{9,... | collective-permute-start | bytes 552968 | tf_op jit(solution)/shard_map/ppermute | solution.py:351
  44.4 0.5 collective-permute-start.13
  44.9 1.5 %collective-permute-start.12 = (bf16[45,16,128]{2,1,0:T(8,128)(2,1)S(1)}, bf16[45,16,128]{2,1,0:T(8,128)(2,1)S(1)}, u32[]{:S(2)}, u32[]{:S(2)}) collective-permute-start(bf16[45,16,128]{2,1,0:T(8,128)(2,1)S(1)} %shard_map.78.refs_0_), channel_id=1, source_target_pairs={{0,1},{1,0},{2,3},{3,2},{4,5},{5,4},{6,7},{7,6},{8,9},{9,8},{10,11... | collective-permute-start | bytes 552968 | tf_op jit(solution)/shard_map/ppermute | solution.py:351
  46.4 0.0 collective-permute-start.15
  46.4 3.0 %collective-permute-done.14.refs_3_ = bf16[45,16,128]{2,1,0:T(8,128)(2,1)S(1)} collective-permute-done((bf16[45,16,128]{2,1,0:T(8,128)(2,1)S(1)}, bf16[45,16,128]{2,1,0:T(8,128)(2,1)S(1)}, u32[]{:S(2)}, u32[]{:S(2)}) %collective-permute-start.14) | collective-permute-done | bytes 184352 | tf_op jit(solution)/shard_map/ppermute | solution.py:351
  49.5 0.0 collective-permute-start.18
  49.5 0.9 %collective-permute-done.13.refs_2_ = bf16[45,16,128]{2,1,0:T(8,128)(2,1)S(1)} collective-permute-done((bf16[45,16,128]{2,1,0:T(8,128)(2,1)S(1)}, bf16[45,16,128]{2,1,0:T(8,128)(2,1)S(1)}, u32[]{:S(2)}, u32[]{:S(2)}) %collective-permute-start.13) | collective-permute-done | bytes 184352 | tf_op jit(solution)/shard_map/ppermute | solution.py:351
  50.4 0.0 collective-permute-start.17
  50.4 0.9 %collective-permute-done.12.refs_1_ = bf16[45,16,128]{2,1,0:T(8,128)(2,1)S(1)} collective-permute-done((bf16[45,16,128]{2,1,0:T(8,128)(2,1)S(1)}, bf16[45,16,128]{2,1,0:T(8,128)(2,1)S(1)}, u32[]{:S(2)}, u32[]{:S(2)}) %collective-permute-start.12) | collective-permute-done | bytes 184352 | tf_op jit(solution)/shard_map/ppermute | solution.py:351
  51.4 0.0 collective-permute-start.16
  51.4 1.1 %shard_map.79 = (bf16[800,800]{1,0:T(8,128)(2,1)}, f32[200,100]{1,0:T(8,128)S(1)}) custom-call(bf16[45,16,128]{2,1,0:T(8,128)(2,1)S(1)} %shard_map.78.refs_0_, bf16[45,16,128]{2,1,0:T(8,128)(2,1)S(1)} %collective-permute-done.12.refs_1_, bf16[45,16,128]{2,1,0:T(8,128)(2,1)S(1)} %collective-permute-done.13.refs_2_, ...), custom_call_target="tpu_custom_call" | custom-call | tf_op jit(solution)/shard_map/pallas_call | solution.py:332
  52.5 0.0 collective-permute-done.15.refs_2_
  52.5 0.0 collective-permute-done.18.refs_5_
  52.5 0.0 collective-permute-done.17.refs_4_
  52.5 0.3 collective-permute-done.16.refs_3_
  52.8 1.8 %shard_map.80 = (bf16[800,800]{1,0:T(8,128)(2,1)}, f32[200,100]{1,0:T(8,128)}, f32[200,100]{1,0:T(8,128)}) custom-call(bf16[800,800]{1,0:T(8,128)(2,1)} %get-tuple-element.52.refs_0_, f32[200,100]{1,0:T(8,128)S(1)} %get-tuple-element.53.refs_1_, bf16[45,16,128]{2,1,0:T(8,128)(2,1)S(1)} %collective-permute-done.15.refs_2_, ...), custom_call_target="tpu_custom_call", output_to_operand_aliasing={{0}: (0, {})} | custom-call | tf_op jit(solution)/shard_map/pallas_call | solution.py:332
  (1 shorter events, 0.0 us)
Async XLA Ops:
  4.0 2.2 %collective-permute-start.1 = (bf16[2,2,20,16,128]{4,3,2,1,0:T(8,128)(2,1)S(1)}, bf16[2,2,20,16,128]{4,3,2,1,0:T(8,128)(2,1)S(1)}, u32[]{:S(2)}, u32[]{:S(2)}) collective-permute-start(bf16[2,2,20,16,128]{4,3,2,1,0:T(8,128)(2,1)S(1)} %get-tuple-element.35), channel_id=1, source_target_pairs={{0,8},{1,9},{2,10},{3,11},{4,12},{5,13},{6,14},{7,15},{8,0},{9,1},... | collective-permute-start | bytes 983048 | tf_op jit(solution)/shard_map/ppermute | solution.py:351
  6.2 1.7 %collective-permute-start = (bf16[2,2,20,16,128]{4,3,2,1,0:T(8,128)(2,1)S(1)}, bf16[2,2,20,16,128]{4,3,2,1,0:T(8,128)(2,1)S(1)}, u32[]{:S(2)}, u32[]{:S(2)}) collective-permute-start(bf16[2,2,20,16,128]{4,3,2,1,0:T(8,128)(2,1)S(1)} %get-tuple-element.33.after_ref), channel_id=1, source_target_pairs={{0,8},{1,9},{2,10},{3,11},{4,12},{5,13},{6,14},{7,15},{8,0},{9,1},... | collective-permute-start | bytes 983048 | tf_op jit(solution)/shard_map/ppermute | solution.py:351
  9.3 6.0 %collective-permute-start.5 = (bf16[4,20,16,128]{3,2,1,0:T(8,128)(2,1)S(1)}, bf16[4,20,16,128]{3,2,1,0:T(8,128)(2,1)S(1)}, u32[]{:S(2)}, u32[]{:S(2)}) collective-permute-start(bf16[4,20,16,128]{3,2,1,0:T(8,128)(2,1)S(1)} %shard_map.71.refs_1_), channel_id=1, source_target_pairs={{0,8},{1,9},{2,10},{3,11},{4,12},{5,13},{6,14},{7,15},{8,0},{9,1},... | collective-permute-start | bytes 983048 | tf_op jit(solution)/shard_map/ppermute | solution.py:351
  9.5 9.4 %collective-permute-start.4 = (bf16[2,20,16,128]{3,2,1,0:T(8,128)(2,1)S(1)}, bf16[2,20,16,128]{3,2,1,0:T(8,128)(2,1)S(1)}, u32[]{:S(2)}, u32[]{:S(2)}) collective-permute-start(bf16[2,20,16,128]{3,2,1,0:T(8,128)(2,1)S(1)} %get-tuple-element.39), channel_id=1, source_target_pairs={{0,16},{1,17},{2,18},{3,19},{4,20},{5,21},{6,22},{7,23},{8,24},{9,... | collective-permute-start | bytes 491528 | tf_op jit(solution)/shard_map/ppermute | solution.py:351
  12.4 10.1 %collective-permute-start.3 = (bf16[2,20,16,128]{3,2,1,0:T(8,128)(2,1)S(1)}, bf16[2,20,16,128]{3,2,1,0:T(8,128)(2,1)S(1)}, u32[]{:S(2)}, u32[]{:S(2)}) collective-permute-start(bf16[2,20,16,128]{3,2,1,0:T(8,128)(2,1)S(1)} %get-tuple-element.38), channel_id=1, source_target_pairs={{0,17},{1,16},{2,19},{3,18},{4,21},{5,20},{6,23},{7,22},{8,25},{9,... | collective-permute-start | bytes 491528 | tf_op jit(solution)/shard_map/ppermute | solution.py:351
  13.9 11.8 %collective-permute-start.2 = (bf16[2,20,16,128]{3,2,1,0:T(8,128)(2,1)S(1)}, bf16[2,20,16,128]{3,2,1,0:T(8,128)(2,1)S(1)}, u32[]{:S(2)}, u32[]{:S(2)}) collective-permute-start(bf16[2,20,16,128]{3,2,1,0:T(8,128)(2,1)S(1)} %get-tuple-element.36.after_ref), channel_id=1, source_target_pairs={{0,1},{1,0},{2,3},{3,2},{4,5},{5,4},{6,7},{7,6},{8,9},{9,8},{10,11... | collective-permute-start | bytes 491528 | tf_op jit(solution)/shard_map/ppermute | solution.py:351
  15.3 23.7 %copy-start = (f32[800,200]{0,1:T(8,128)S(1)}, f32[800,200]{0,1:T(8,128)}, u32[]{:S(2)}) copy-start(f32[800,200]{0,1:T(8,128)} %param.6) | copy-start | bytes 1920004
  15.3 23.7 %copy-start.1 = (f32[800,200]{0,1:T(8,128)S(1)}, f32[800,200]{0,1:T(8,128)}, u32[]{:S(2)}) copy-start(f32[800,200]{0,1:T(8,128)} %param.7) | copy-start | bytes 1920004
  15.4 12.0 %collective-permute-start.7 = (bf16[20,16,128]{2,1,0:T(8,128)(2,1)S(1)}, bf16[20,16,128]{2,1,0:T(8,128)(2,1)S(1)}, u32[]{:S(2)}, u32[]{:S(2)}) collective-permute-start(bf16[20,16,128]{2,1,0:T(8,128)(2,1)S(1)} %get-tuple-element.43), channel_id=1, source_target_pairs={{0,1},{1,0},{2,3},{3,2},{4,5},{5,4},{6,7},{7,6},{8,9},{9,8},{10,11... | collective-permute-start | bytes 245768 | tf_op jit(solution)/shard_map/ppermute | solution.py:351
  17.4 10.0 %collective-permute-start.8 = (bf16[20,16,128]{2,1,0:T(8,128)(2,1)S(1)}, bf16[20,16,128]{2,1,0:T(8,128)(2,1)S(1)}, u32[]{:S(2)}, u32[]{:S(2)}) collective-permute-start(bf16[20,16,128]{2,1,0:T(8,128)(2,1)S(1)} %get-tuple-element.44), channel_id=1, source_target_pairs={{0,16},{1,17},{2,18},{3,19},{4,20},{5,21},{6,22},{7,23},{8,24},{9,... | collective-permute-start | bytes 245768 | tf_op jit(solution)/shard_map/ppermute | solution.py:351
  18.9 8.5 %collective-permute-start.9 = (bf16[20,16,128]{2,1,0:T(8,128)(2,1)S(1)}, bf16[20,16,128]{2,1,0:T(8,128)(2,1)S(1)}, u32[]{:S(2)}, u32[]{:S(2)}) collective-permute-start(bf16[20,16,128]{2,1,0:T(8,128)(2,1)S(1)} %get-tuple-element.45), channel_id=1, source_target_pairs={{0,17},{1,16},{2,19},{3,18},{4,21},{5,20},{6,23},{7,22},{8,25},{9,... | collective-permute-start | bytes 245768 | tf_op jit(solution)/shard_map/ppermute | solution.py:351
  25.8 5.2 %collective-permute-start.6 = (bf16[20,16,128]{2,1,0:T(8,128)(2,1)S(1)}, bf16[20,16,128]{2,1,0:T(8,128)(2,1)S(1)}, u32[]{:S(2)}, u32[]{:S(2)}) collective-permute-start(bf16[20,16,128]{2,1,0:T(8,128)(2,1)S(1)} %get-tuple-element.42), channel_id=1, source_target_pairs={{0,2},{1,3},{2,0},{3,1},{4,6},{5,7},{6,4},{7,5},{8,10},{9,11},{10,... | collective-permute-start | bytes 245768 | tf_op jit(solution)/shard_map/ppermute | solution.py:351
  31.1 6.0 %collective-permute-start.10 = (bf16[30,16,128]{2,1,0:T(8,128)(2,1)S(1)}, bf16[30,16,128]{2,1,0:T(8,128)(2,1)S(1)}, u32[]{:S(2)}, u32[]{:S(2)}) collective-permute-start(bf16[30,16,128]{2,1,0:T(8,128)(2,1)S(1)} %get-tuple-element.46.refs_0_), channel_id=1, source_target_pairs={{0,4},{1,5},{2,6},{3,7},{4,0},{5,1},{6,2},{7,3},{8,12},{9,13},{10,... | collective-permute-start | bytes 368648 | tf_op jit(solution)/shard_map/ppermute | solution.py:351
  37.1 4.7 %collective-permute-start.11 = (bf16[25,16,128]{2,1,0:T(8,128)(2,1)S(1)}, bf16[25,16,128]{2,1,0:T(8,128)(2,1)S(1)}, u32[]{:S(2)}, u32[]{:S(2)}) collective-permute-start(bf16[25,16,128]{2,1,0:T(8,128)(2,1)S(1)} %get-tuple-element.48.refs_0_), channel_id=1, source_target_pairs={{0,2},{1,3},{2,0},{3,1},{4,6},{5,7},{6,4},{7,5},{8,10},{9,11},{10,... | collective-permute-start | bytes 307208 | tf_op jit(solution)/shard_map/ppermute | solution.py:351
  42.9 6.6 %collective-permute-start.14 = (bf16[45,16,128]{2,1,0:T(8,128)(2,1)S(1)}, bf16[45,16,128]{2,1,0:T(8,128)(2,1)S(1)}, u32[]{:S(2)}, u32[]{:S(2)}) collective-permute-start(bf16[45,16,128]{2,1,0:T(8,128)(2,1)S(1)} %shard_map.78.refs_0_), channel_id=1, source_target_pairs={{0,17},{1,16},{2,19},{3,18},{4,21},{5,20},{6,23},{7,22},{8,25},{9,... | collective-permute-start | bytes 552968 | tf_op jit(solution)/shard_map/ppermute | solution.py:351
  44.4 6.0 %collective-permute-start.13 = (bf16[45,16,128]{2,1,0:T(8,128)(2,1)S(1)}, bf16[45,16,128]{2,1,0:T(8,128)(2,1)S(1)}, u32[]{:S(2)}, u32[]{:S(2)}) collective-permute-start(bf16[45,16,128]{2,1,0:T(8,128)(2,1)S(1)} %shard_map.78.refs_0_), channel_id=1, source_target_pairs={{0,16},{1,17},{2,18},{3,19},{4,20},{5,21},{6,22},{7,23},{8,24},{9,... | collective-permute-start | bytes 552968 | tf_op jit(solution)/shard_map/ppermute | solution.py:351
  44.9 6.4 %collective-permute-start.12 = (bf16[45,16,128]{2,1,0:T(8,128)(2,1)S(1)}, bf16[45,16,128]{2,1,0:T(8,128)(2,1)S(1)}, u32[]{:S(2)}, u32[]{:S(2)}) collective-permute-start(bf16[45,16,128]{2,1,0:T(8,128)(2,1)S(1)} %shard_map.78.refs_0_), channel_id=1, source_target_pairs={{0,1},{1,0},{2,3},{3,2},{4,5},{5,4},{6,7},{7,6},{8,9},{9,8},{10,11... | collective-permute-start | bytes 552968 | tf_op jit(solution)/shard_map/ppermute | solution.py:351
  46.4 6.0 %collective-permute-start.15 = (bf16[45,16,128]{2,1,0:T(8,128)(2,1)S(1)}, bf16[45,16,128]{2,1,0:T(8,128)(2,1)S(1)}, u32[]{:S(2)}, u32[]{:S(2)}) collective-permute-start(bf16[45,16,128]{2,1,0:T(8,128)(2,1)S(1)} %shard_map.78.refs_0_), channel_id=1, source_target_pairs={{0,8},{1,9},{2,10},{3,11},{4,12},{5,13},{6,14},{7,15},{8,0},{9,1},... | collective-permute-start | bytes 552968 | tf_op jit(solution)/shard_map/ppermute | solution.py:351
  49.5 3.0 %collective-permute-start.18 = (bf16[45,16,128]{2,1,0:T(8,128)(2,1)S(1)}, bf16[45,16,128]{2,1,0:T(8,128)(2,1)S(1)}, u32[]{:S(2)}, u32[]{:S(2)}) collective-permute-start(bf16[45,16,128]{2,1,0:T(8,128)(2,1)S(1)} %collective-permute-done.14.refs_3_), channel_id=1, source_target_pairs={{0,8},{1,9},{2,10},{3,11},{4,12},{5,13},{6,14},{7,15},{8,0},{9,1},... | collective-permute-start | bytes 552968 | tf_op jit(solution)/shard_map/ppermute | solution.py:351
  50.4 2.1 %collective-permute-start.17 = (bf16[45,16,128]{2,1,0:T(8,128)(2,1)S(1)}, bf16[45,16,128]{2,1,0:T(8,128)(2,1)S(1)}, u32[]{:S(2)}, u32[]{:S(2)}) collective-permute-start(bf16[45,16,128]{2,1,0:T(8,128)(2,1)S(1)} %collective-permute-done.13.refs_2_), channel_id=1, source_target_pairs={{0,8},{1,9},{2,10},{3,11},{4,12},{5,13},{6,14},{7,15},{8,0},{9,1},... | collective-permute-start | bytes 552968 | tf_op jit(solution)/shard_map/ppermute | solution.py:351
  51.4 1.4 %collective-permute-start.16 = (bf16[45,16,128]{2,1,0:T(8,128)(2,1)S(1)}, bf16[45,16,128]{2,1,0:T(8,128)(2,1)S(1)}, u32[]{:S(2)}, u32[]{:S(2)}) collective-permute-start(bf16[45,16,128]{2,1,0:T(8,128)(2,1)S(1)} %collective-permute-done.12.refs_1_), channel_id=1, source_target_pairs={{0,8},{1,9},{2,10},{3,11},{4,12},{5,13},{6,14},{7,15},{8,0},{9,1},... | collective-permute-start | bytes 552968 | tf_op jit(solution)/shard_map/ppermute | solution.py:351
